TPU v7x, 32 devices: a whole 2x2x4 slice. The times are simulated.
32 devices in a mesh: dp: 8 (over z, y), tensor: 4 (over x, core).
Axes of the slice: x: 2, y: 2, z: 4, core: 2. Of those that a mesh axis runs over, the one named last changes fastest.
Arguments:
- clean_latents: bfloat16 [8, 512, 2048], P('dp', 'tensor'), may hold values from -24 to 24
- noise_latents: bfloat16 [8, 512, 2048], P('dp', 'tensor'), may hold values from -24 to 24
- step_index: int32 [8], P('dp'), may hold values from 0 to 999
- labels: int32 [8], P('dp'), may hold values from 0 to 999
- class_shift: bfloat16 [1000, 2048], replicated, may hold values from -6 to 6
- w_qkv: bfloat16 [2048, 3072], P('dp', 'tensor'), may hold values from -0.2 to 0.2
- w_out_t: bfloat16 [2048, 1024], P('dp', 'tensor'), may hold values from -0.1875 to 0.1875
Outputs:
- grad_qkv: float32 [2048, 3072], P('dp', 'tensor')
- grad_out: float32 [2048, 1024], P('dp', 'tensor')
All inputs are finite; a program needn't handle non-finite values.
Results may differ from a plain program's by a relative error of at most 0.0075.
Values may be sent and summed in bfloat16 or wider, within the bound.
A program may use at most 128 MiB of HBM per device.

v0:
```python
import math

import jax
import jax.numpy as jnp
from jax import lax
from jax.sharding import PartitionSpec as P

HEAD_DIM = 128
STEPS = 1000


norm_eps = 1e-06
target_floor = 0.1


def time_terms(step_index, model_width):
    step_times = 1.4 * (step_index.astype(jnp.float32) + 0.5) / STEPS
    feature_ids = jnp.arange(model_width, dtype=jnp.float32)
    frequency = jnp.exp(-math.log(100.0) * feature_ids / model_width)
    phases = step_times[:, None] * frequency[None, :] + feature_ids[None, :]
    return (step_times, 0.5 * jnp.sin(phases), 0.5 * frequency[None, :] * jnp.cos(phases))


def trig_path(clean_part, noise_part, step_times):
    cos_t = jnp.cos(step_times)[:, None, None]
    sin_t = jnp.sin(step_times)[:, None, None]
    clean_wide = clean_part.astype(jnp.float32)
    noise_wide = noise_part.astype(jnp.float32)
    return (cos_t * clean_wide + sin_t * noise_wide, cos_t * noise_wide - sin_t * clean_wide)


def modulate(noisy, velocity, amplitude, amp_rate, class_offset):
    inverse = lax.rsqrt(jnp.mean(noisy * noisy, axis=-1, keepdims=True) + norm_eps)
    normed = noisy * inverse
    normed_rate = velocity * inverse - noisy * inverse**3 * jnp.mean(
        noisy * velocity, axis=-1, keepdims=True
    )
    scale_up = 1.0 + amplitude[:, None, :]
    mixed = normed * scale_up + class_offset[:, None, :]
    mixed_rate = normed_rate * scale_up + normed * amp_rate[:, None, :]
    return (mixed.astype(jnp.bfloat16), mixed_rate.astype(jnp.bfloat16))


def target_of(noisy, velocity, proj, proj_rate, step_times):
    cos_t = jnp.cos(step_times)[:, None, None]
    sin_t = jnp.sin(step_times)[:, None, None]
    model_out = noisy + proj
    model_rate = velocity + proj_rate
    return -(cos_t * cos_t) * (model_out - velocity) - cos_t * sin_t * (noisy + model_rate)


def low_einsum(form, left_part, right_part):
    return jnp.einsum(form, left_part, right_part, preferred_element_type=jnp.float32)


def attend(projected, projected_rate, score_scale):
    query_part = projected[:, :, :, 0, :]
    key_part = projected[:, :, :, 1, :]
    value_part = projected[:, :, :, 2, :]
    query_rate = projected_rate[:, :, :, 0, :]
    key_rate = projected_rate[:, :, :, 1, :]
    value_rate = projected_rate[:, :, :, 2, :]
    scores = low_einsum("lqhd,lkhd->lhqk", query_part, key_part) * score_scale
    score_rate = (
        low_einsum("lqhd,lkhd->lhqk", query_rate, key_part)
        + low_einsum("lqhd,lkhd->lhqk", query_part, key_rate)
    ) * score_scale
    attn_probs = jax.nn.softmax(scores, axis=-1)
    probs_low = attn_probs.astype(jnp.bfloat16)
    prob_rate = attn_probs * (score_rate - jnp.sum(attn_probs * score_rate, axis=-1, keepdims=True))
    prob_rate_low = prob_rate.astype(jnp.bfloat16)
    attn_out = low_einsum("lhqk,lkhd->lqhd", probs_low, value_part)
    attn_rate = low_einsum("lhqk,lkhd->lqhd", prob_rate_low, value_part) + low_einsum(
        "lhqk,lkhd->lqhd", probs_low, value_rate
    )
    return (attn_probs, probs_low, attn_out.astype(jnp.bfloat16), attn_rate.astype(jnp.bfloat16))


def attend_back(attn_grad, attn_probs, probs_low, projected, score_scale):
    query_part = projected[:, :, :, 0, :]
    key_part = projected[:, :, :, 1, :]
    value_part = projected[:, :, :, 2, :]
    prob_grad = low_einsum("lqhd,lkhd->lhqk", attn_grad, value_part)
    value_grad = low_einsum("lhqk,lqhd->lkhd", probs_low, attn_grad)
    score_grad = (
        attn_probs
        * (prob_grad - jnp.sum(attn_probs * prob_grad, axis=-1, keepdims=True))
        * score_scale
    ).astype(jnp.bfloat16)
    query_grad = low_einsum("lhqk,lkhd->lqhd", score_grad, key_part)
    key_grad = low_einsum("lhqk,lqhd->lkhd", score_grad, query_part)
    return jnp.stack([query_grad, key_grad, value_grad], axis=3).astype(jnp.bfloat16)


def row_contract(left_part, right_part):
    return lax.dot_general(
        left_part, right_part, (((0,), (0,)), ((), ())), preferred_element_type=jnp.float32
    )


def local(clean_latents, noise_latents, step_index, labels, class_shift, w_qkv, w_out_t):
    latent_count, part_len, model_width = clean_latents.shape
    class_count = class_shift.shape[0]
    head_cols = w_out_t.shape[1]
    heads_here = head_cols // HEAD_DIM
    score_scale = 1.0 / math.sqrt(HEAD_DIM)
    step_times, amplitude, amp_rate = time_terms(step_index, model_width)
    one_hot = (labels[:, None] == jnp.arange(class_count, dtype=jnp.int32)[None, :]).astype(
        jnp.bfloat16
    )
    class_offset = jnp.dot(one_hot, class_shift, preferred_element_type=jnp.float32)
    clean_all, noise_all = (
        lax.all_gather(clean_latents, "tensor", axis=1, tiled=True),
        lax.all_gather(noise_latents, "tensor", axis=1, tiled=True),
    )
    seq_len = clean_all.shape[1]
    row_count = latent_count * seq_len
    loss_scale = 1.0 / math.sqrt(lax.axis_size("dp") * latent_count * seq_len)
    noisy_all, velocity_all = trig_path(clean_all, noise_all, step_times)
    mixed, mixed_rate = modulate(noisy_all, velocity_all, amplitude, amp_rate, class_offset)
    mixed_rows = mixed.reshape(row_count, model_width)
    rate_rows = mixed_rate.reshape(row_count, model_width)
    qkv_all, out_all = (
        lax.all_gather(w_qkv, "dp", axis=0, tiled=True),
        lax.all_gather(w_out_t, "dp", axis=0, tiled=True),
    )
    projected = jnp.dot(mixed_rows, qkv_all, preferred_element_type=jnp.float32)
    projected_rate = jnp.dot(rate_rows, qkv_all, preferred_element_type=jnp.float32)
    projected = projected.astype(jnp.bfloat16).reshape(
        latent_count, seq_len, heads_here, 3, HEAD_DIM
    )
    projected_rate = projected_rate.astype(jnp.bfloat16).reshape(
        latent_count, seq_len, heads_here, 3, HEAD_DIM
    )
    attn_probs, probs_low, attn_out, attn_rate = attend(projected, projected_rate, score_scale)
    attn_rows = attn_out.reshape(row_count, head_cols)
    paired = jnp.stack([attn_rows, attn_rate.reshape(row_count, head_cols)])
    head_sums = lax.dot_general(
        paired, out_all, (((2,), (1,)), ((), ())), preferred_element_type=jnp.float32
    )
    head_sums = head_sums.reshape(2, latent_count, seq_len, model_width)
    own_sums = lax.psum_scatter(head_sums, "tensor", scatter_dimension=2, tiled=True)
    noisy_own, velocity_own = trig_path(clean_latents, noise_latents, step_times)
    target = target_of(noisy_own, velocity_own, own_sums[0], own_sums[1], step_times)
    squares = lax.psum(jnp.sum(target * target, axis=(1, 2)), "tensor")
    spread = jnp.sqrt(squares / (seq_len * model_width))
    own_cot = (-(target / (spread[:, None, None] + target_floor)) * loss_scale).astype(jnp.bfloat16)
    cotangent = lax.all_gather(own_cot, "tensor", axis=1, tiled=True)
    cot_rows = cotangent.reshape(row_count, model_width)
    out_partial = row_contract(cot_rows, attn_rows)
    attn_grad = jnp.dot(cot_rows, out_all, preferred_element_type=jnp.float32)
    attn_grad = attn_grad.astype(jnp.bfloat16).reshape(latent_count, seq_len, heads_here, HEAD_DIM)
    qkv_grad = attend_back(attn_grad, attn_probs, probs_low, projected, score_scale).reshape(
        row_count, 3 * head_cols
    )
    in_partial = row_contract(mixed_rows, qkv_grad)
    grad_qkv, grad_out = (
        lax.psum_scatter(in_partial, "dp", scatter_dimension=0, tiled=True),
        lax.psum_scatter(out_partial, "dp", scatter_dimension=0, tiled=True),
    )
    return (grad_qkv, grad_out)


def solution(mesh):
    in_specs = (
        P("dp", "tensor", None),
        P("dp", "tensor", None),
        P("dp"),
        P("dp"),
        P(),
        P("dp", "tensor"),
        P("dp", "tensor"),
    )
    out_specs = (P("dp", "tensor"), P("dp", "tensor"))
    return jax.shard_map(local, mesh=mesh, in_specs=in_specs, out_specs=out_specs, check_vma=False)
```

profile of v0, /device:TPU:0, one launch (start us, length us, event | category | flops | bytes accessed | tf_op | source)
XLA Modules:
  0.0 472.9 jit_solution(5457915576163600078)
XLA Ops:
  7.9 0.7 all-gather.8.cloned.1.call-update
  11.6 2.9 fusion.99
  14.5 20.4 %all-gather.6.cloned.1.call-done = bf16[1,512,2048]{2,1,0:T(8,128)(2,1)} async-done(((bf16[1,128,2048]{2,1,0:T(8,128)(2,1)}), bf16[1,512,2048]{2,1,0:T(8,128)(2,1)}) %all-gather.6.cloned.1.call-update) | async-done | bytes 2097168 | tf_op jit(solution)/shard_map/all_gather | solution.py:113
  34.8 24.2 %all-gather.8.cloned.1.call-done = bf16[1,512,2048]{2,1,0:T(8,128)(2,1)} async-done(((bf16[1,128,2048]{2,1,0:T(8,128)(2,1)}), bf16[1,512,2048]{2,1,0:T(8,128)(2,1)}) %all-gather.8.cloned.1.call-update) | async-done | bytes 2097168 | tf_op jit(solution)/shard_map/all_gather | solution.py:114
  59.0 4.8 %multiply_reduce_fusion.1 = (f32[512]{0:T(512)S(1)}, f32[512]{0:T(512)S(1)}) fusion(bf16[1,512,2048]{2,1,0:T(8,128)(2,1)} %all-gather.8.cloned.1.call-done, f32[]{:T(128)} %bitcast.1, bf16[1,512,2048]{2,1,0:T(8,128)(2,1)} %all-gather.6.cloned.1.call-done, f32[]{:T(128)} %bitcast), kind=kLoop, calls=%fused_computation.12 | loop fusion | flops 12581888 | bytes 4198408 | tf_op jit(solution)/shard_map/reduce_sum | solution.py:33
  63.8 57.5 %all-gather.10.cloned.1.call-done = bf16[2048,768]{1,0:T(8,128)(2,1)} async-done(((bf16[256,768]{1,0:T(8,128)(2,1)}), bf16[2048,768]{1,0:T(8,128)(2,1)}) %all-gather.10.cloned.1.call-update) | async-done | bytes 3145744 | tf_op jit(solution)/shard_map/all_gather | solution.py:124
  121.2 6.2 %fusion.28 = bf16[512,768]{1,0:T(8,128)(2,1)S(1)} fusion(bf16[2048,768]{1,0:T(8,128)(2,1)} %all-gather.10.cloned.1.call-done, f32[2048]{0:T(1024)S(1)} %get-tuple-element.12, bf16[1,512,2048]{2,1,0:T(8,128)(2,1)S(1)} %copy-done.1, bf16[1,512,2048]{2,1,0:T(8,128)(2,1)} %all-gather.8.cloned.1.call-done, f32[512]{0:T(512)S(1)} %get-tuple-element.14, ...), kind=kOutput, calls=%fused_computation.38 | convolution fusion | flops 1628831744 | bytes 8149000 | tf_op jit(solution)/shard_map/dot_general | solution.py:128
  127.5 3.3 convolution_convert_fusion
  131.1 1.4 copy.28
  132.5 2.2 fusion.98
  135.2 1.1 copy-done.8
  136.3 1.9 multiply_reduce_fusion.3
  138.3 3.0 fusion.50
  141.3 1.4 fusion.31
  142.8 1.2 convolution_convert_fusion.2
  144.1 18.1 %all-gather.12.cloned.1.call-done = bf16[2048,256]{1,0:T(8,128)(2,1)} async-done(((bf16[256,256]{1,0:T(8,128)(2,1)}), bf16[2048,256]{1,0:T(8,128)(2,1)}) %all-gather.12.cloned.1.call-update) | async-done | bytes 1048592 | tf_op jit(solution)/shard_map/all_gather | solution.py:125
  162.2 5.7 %convolution_bitcast_fusion = f32[2,1,512,2048]{3,2,0,1:T(8,128)} fusion(bf16[2048,256]{1,0:T(8,128)(2,1)} %all-gather.12.cloned.1.call-done, bf16[1,512,256]{2,1,0:T(8,128)(2,1)S(1)} %copy.40, bf16[1,512,256]{2,1,0:T(8,128)(2,1)S(1)} %copy.39), kind=kOutput, calls=%fused_computation.6 | convolution fusion | flops 1074003968 | bytes 9961472 | tf_op jit(solution)/shard_map/dot_general | solution.py:138
  168.0 70.2 %reduce-scatter.4.cloned.1.call-done = f32[2,1,128,2048]{3,2,0,1:T(8,128)} async-done(((f32[2,1,512,2048]{3,2,0,1:T(8,128)}), f32[2,1,128,2048]{3,2,0,1:T(8,128)}) %reduce-scatter.4.cloned.1.call-update) | async-done | bytes 2097168 | tf_op jit(solution)/shard_map/reduce_scatter | solution.py:142
  238.2 2.8 multiply_reduce_fusion.5
  241.0 6.4 %psum.7 = f32[1]{0:T(128)} all-reduce(f32[1]{0:T(128)} %bitcast.28), channel_id=1, replica_groups=mesh['dp'=8,'tensor'=4] {'tensor'}, use_global_device_ids=true, to_apply=%region_7.0 | all-reduce | flops 1 | bytes 8 | tf_op jit(solution)/shard_map/psum | solution.py:145
  248.1 0.9 multiply_convert_fusion.3
  249.1 23.3 %all-gather.14.cloned.1.call-done = bf16[1,512,2048]{2,1,0:T(8,128)(2,1)} async-done(((bf16[1,128,2048]{2,1,0:T(8,128)(2,1)}), bf16[1,512,2048]{2,1,0:T(8,128)(2,1)}) %all-gather.14.cloned.1.call-update) | async-done | bytes 2097168 | tf_op jit(solution)/shard_map/all_gather | solution.py:148
  272.4 3.7 fusion.5
  276.2 1.5 copy-done
  277.7 2.0 fusion.38
  280.1 3.2 fusion.44
  283.4 3.8 fusion.41
  287.2 1.9 fusion.47
  289.1 1.3 pad_maximum_fusion
  290.9 5.5 %fusion.78 = f32[2048,768]{1,0:T(8,128)} fusion(bf16[512,768]{0,1:T(8,128)(2,1)S(1)} %bitcast.201, f32[2048]{0:T(1024)S(1)} %bitcast.206, f32[2048]{0:T(1024)S(1)} %get-tuple-element.13, f32[512]{0:T(512)S(1)} %get-tuple-element.6, bf16[1,512,2048]{2,1,0:T(8,128)(2,1)S(1)} %copy-done.4, f32[]{:T(128)} %bitcast.1, bf16[1,512,2048]{2,1,0:T(8,128)(2,1)S(1)} %copy-done.2, ...), kind=kOutput, calls=%fused_computation.103 | convolution fusion | flops 1620049920 | bytes 11290632 | tf_op jit(solution)/shard_map/dot_general | solution.py:96
  296.5 48.4 %reduce-scatter.8.cloned.1.call-done = f32[256,256]{1,0:T(8,128)} async-done(((f32[2048,256]{1,0:T(8,128)}), f32[256,256]{1,0:T(8,128)}) %reduce-scatter.8.cloned.1.call-update) | async-done | bytes 262160 | tf_op jit(solution)/shard_map/reduce_scatter | solution.py:159
  344.9 121.2 %reduce-scatter.6.cloned.1.call-done = f32[256,768]{1,0:T(8,128)} async-done(((f32[2048,768]{1,0:T(8,128)}), f32[256,768]{1,0:T(8,128)}) %reduce-scatter.6.cloned.1.call-update) | async-done | bytes 786448 | tf_op jit(solution)/shard_map/reduce_scatter | solution.py:158
  (41 shorter events, 4.4 us)
Async XLA Ops:
  7.2 27.7 %all-gather.6.cloned.1.call-start = ((), (), s32[]{:S(2)}) async-start(), calls=%async_computation.3 | async-start | bytes 2621440 | tf_op jit(solution)/shard_map/all_gather | solution.py:113
  7.9 51.1 %all-gather.8.cloned.1.call-start = ((), (), s32[]{:S(2)}) async-start(), calls=%async_computation.4 | async-start | bytes 2621440 | tf_op jit(solution)/shard_map/all_gather | solution.py:114
  8.6 112.6 %all-gather.10.cloned.1.call-start = ((), (), s32[]{:S(2)}) async-start(), calls=%async_computation.5 | async-start | bytes 3538944 | tf_op jit(solution)/shard_map/all_gather | solution.py:124
  9.4 152.8 %all-gather.12.cloned.1.call-start = ((), (), s32[]{:S(2)}) async-start(), calls=%async_computation.6 | async-start | bytes 1179648 | tf_op jit(solution)/shard_map/all_gather | solution.py:125
  10.0 228.3 %reduce-scatter.4.cloned.1.call-start = ((), (), s32[]{:S(2)}) async-start(), calls=%async_computation.7 | async-start | bytes 10485760 | tf_op jit(solution)/shard_map/reduce_scatter | solution.py:142
  59.0 62.2 %copy-start.1 = (bf16[1,512,2048]{2,1,0:T(8,128)(2,1)S(1)}, bf16[1,512,2048]{2,1,0:T(8,128)(2,1)}, u32[]{:S(2)}) copy-start(bf16[1,512,2048]{2,1,0:T(8,128)(2,1)} %all-gather.6.cloned.1.call-done) | copy-start | bytes 6291460
  121.2 6.2 %copy-start.3 = (bf16[1,512,2048]{2,1,0:T(8,128)(2,1)S(1)}, bf16[1,512,2048]{2,1,0:T(8,128)(2,1)}, u32[]{:S(2)}) copy-start(bf16[1,512,2048]{2,1,0:T(8,128)(2,1)} %all-gather.8.cloned.1.call-done) | copy-start | bytes 6291460
  121.2 6.2 %copy-start.7 = (bf16[2048,768]{1,0:T(8,128)(2,1)S(1)}, bf16[2048,768]{1,0:T(8,128)(2,1)}, u32[]{:S(2)}) copy-start(bf16[2048,768]{1,0:T(8,128)(2,1)} %all-gather.10.cloned.1.call-done) | copy-start | bytes 9437188
  134.7 1.6 copy-start.8
  167.9 70.3 %copy-start.5 = (bf16[1,128,2048]{2,1,0:T(8,128)(2,1)S(1)}, bf16[1,128,2048]{2,1,0:T(8,128)(2,1)}, u32[]{:S(2)}) copy-start(bf16[1,128,2048]{2,1,0:T(8,128)(2,1)} %param.7) | copy-start | bytes 1572868
  167.9 70.3 %copy-start.6 = (bf16[1,128,2048]{2,1,0:T(8,128)(2,1)S(1)}, bf16[1,128,2048]{2,1,0:T(8,128)(2,1)}, u32[]{:S(2)}) copy-start(bf16[1,128,2048]{2,1,0:T(8,128)(2,1)} %param.8) | copy-start | bytes 1572868
  168.0 104.4 %all-gather.14.cloned.1.call-start = ((), (), s32[]{:S(2)}) async-start(), calls=%async_computation.8 | async-start | bytes 2621440 | tf_op jit(solution)/shard_map/all_gather | solution.py:148
  249.0 95.9 %reduce-scatter.8.cloned.1.call-start = ((), (), s32[]{:S(2)}) async-start(), calls=%async_computation.10 | async-start | bytes 2359296 | tf_op jit(solution)/shard_map/reduce_scatter | solution.py:159
  276.1 1.6 copy-start
  276.1 190.0 %reduce-scatter.6.cloned.1.call-start = ((), (), s32[]{:S(2)}) async-start(), calls=%async_computation.9 | async-start | bytes 7077888 | tf_op jit(solution)/shard_map/reduce_scatter | solution.py:158
  287.2 3.3 copy-start.4
  289.1 1.8 copy-start.2
Sparse Core Ops, SparseCore 0:
  9.5 25.2 all-gather.5
  36.4 22.5 all-gather.7
  61.2 60.0 all-gather.9
  123.2 38.9 all-gather.11
  168.1 70.0 reduce-scatter.3
  249.1 23.1 all-gather.13
  276.5 68.3 reduce-scatter.7
  349.0 117.0 reduce-scatter.5
where the time goes:
time: 473 us
  waiting for transfers between devices  386 us (82%)
  matrix products  49 us (10%)
  between operations  16.4 us (3%)
  other arithmetic  9.83 us (2%)
  blocking collectives  6.36 us (1%)
  local copies, waits for them, and re-layouts  5.09 us (1%)
    reduce_scatter x1, waiting for transfers between devices, local(): lax.psum_scatter(in_partial, 'dp', scatter_dimension=0, tiled=True)  121 us
    reduce_scatter x1, waiting for transfers between devices, local(): lax.psum_scatter(head_sums, 'tensor', scatter_dimension=2, tiled=True)  70.2 us
    all_gather x1, waiting for transfers between devices, local(): lax.all_gather(w_qkv, 'dp', axis=0, tiled=True)  57.5 us
    reduce_scatter x1, waiting for transfers between devices, local(): lax.psum_scatter(out_partial, 'dp', scatter_dimension=0, tiled=True)  48.4 us
    all_gather x1, waiting for transfers between devices, local(): lax.all_gather(noise_latents, 'tensor', axis=1, tiled=True)  24.2 us
    all_gather x1, waiting for transfers between devices, local(): cotangent = lax.all_gather(own_cot, 'tensor', axis=1, tiled=True)  23.3 us
    all_gather x1, waiting for transfers between devices, local(): lax.all_gather(clean_latents, 'tensor', axis=1, tiled=True)  20.4 us
    all_gather x1, waiting for transfers between devices, local(): lax.all_gather(w_out_t, 'dp', axis=0, tiled=True)  18.1 us
  transfers between devices with their start and end apart: 8, of which 8 were waited for; matrix products, arithmetic and copies ran while one was open for 10% of the time, Pallas kernels for 0%

commit v1 on v0

v1 whole, which is shorter than its diff:
```python
import functools
import math

import jax
import jax.numpy as jnp
from jax import lax
from jax.experimental import pallas as pl
from jax.experimental.pallas import tpu as pltpu
from jax.sharding import PartitionSpec as P

HEAD_DIM = 128
STEPS = 1000


norm_eps = 1e-06
target_floor = 0.1


def time_terms(step_index, model_width):
    step_times = 1.4 * (step_index.astype(jnp.float32) + 0.5) / STEPS
    feature_ids = jnp.arange(model_width, dtype=jnp.float32)
    frequency = jnp.exp(-math.log(100.0) * feature_ids / model_width)
    phases = step_times[:, None] * frequency[None, :] + feature_ids[None, :]
    return (step_times, 0.5 * jnp.sin(phases), 0.5 * frequency[None, :] * jnp.cos(phases))


def low_einsum(form, left_part, right_part):
    return jnp.einsum(form, left_part, right_part, preferred_element_type=jnp.float32)


def attend(projected, projected_rate, score_scale):
    query_part = projected[:, :, :, 0, :]
    key_part = projected[:, :, :, 1, :]
    value_part = projected[:, :, :, 2, :]
    query_rate = projected_rate[:, :, :, 0, :]
    key_rate = projected_rate[:, :, :, 1, :]
    value_rate = projected_rate[:, :, :, 2, :]
    scores = low_einsum("lqhd,lkhd->lhqk", query_part, key_part) * score_scale
    score_rate = (
        low_einsum("lqhd,lkhd->lhqk", query_rate, key_part)
        + low_einsum("lqhd,lkhd->lhqk", query_part, key_rate)
    ) * score_scale
    attn_probs = jax.nn.softmax(scores, axis=-1)
    probs_low = attn_probs.astype(jnp.bfloat16)
    prob_rate = attn_probs * (score_rate - jnp.sum(attn_probs * score_rate, axis=-1, keepdims=True))
    prob_rate_low = prob_rate.astype(jnp.bfloat16)
    attn_out = low_einsum("lhqk,lkhd->lqhd", probs_low, value_part)
    attn_rate = low_einsum("lhqk,lkhd->lqhd", prob_rate_low, value_part) + low_einsum(
        "lhqk,lkhd->lqhd", probs_low, value_rate
    )
    return (attn_probs, probs_low, attn_out, attn_rate)


def attend_back(attn_grad, attn_probs, probs_low, projected, score_scale):
    query_part = projected[:, :, :, 0, :]
    key_part = projected[:, :, :, 1, :]
    value_part = projected[:, :, :, 2, :]
    prob_grad = low_einsum("lqhd,lkhd->lhqk", attn_grad, value_part)
    value_grad = low_einsum("lhqk,lqhd->lkhd", probs_low, attn_grad)
    score_grad = (
        attn_probs
        * (prob_grad - jnp.sum(attn_probs * prob_grad, axis=-1, keepdims=True))
        * score_scale
    ).astype(jnp.bfloat16)
    query_grad = low_einsum("lhqk,lkhd->lqhd", score_grad, key_part)
    key_grad = low_einsum("lhqk,lqhd->lkhd", score_grad, query_part)
    return jnp.stack([query_grad, key_grad, value_grad], axis=3).astype(jnp.bfloat16)


def row_contract(left_part, right_part):
    return lax.dot_general(
        left_part, right_part, (((0,), (0,)), ((), ())), preferred_element_type=jnp.float32
    )


MESH = pl.DeviceIdType.MESH
VMEM = pl.BlockSpec(memory_space=pltpu.VMEM)
HBM = pl.BlockSpec(memory_space=pl.ANY)


def places():
    dp_here, tensor_here = lax.axis_index("dp"), lax.axis_index("tensor")
    sibling = tensor_here + 1 - 2 * lax.rem(tensor_here, 2)
    opposite = lax.rem(tensor_here + 2, 4)
    diagonal = lax.rem(sibling + 2, 4)
    return dp_here, tensor_here, sibling, opposite, diagonal


def greet(devices):
    barrier = pltpu.get_barrier_semaphore()
    for device in devices:
        pl.semaphore_signal(barrier, inc=1, device_id=device, device_id_type=MESH)
    pl.semaphore_wait(barrier, len(devices))


def remote(source, target, send_sem, recv_sem, device):
    return pltpu.make_async_remote_copy(
        src_ref=source,
        dst_ref=target,
        send_sem=send_sem,
        recv_sem=recv_sem,
        device_id=device,
        device_id_type=MESH,
    )


def rows_of(ref, index, count):
    return ref.at[pl.ds(pl.multiple_of(index * count, count), count)]


def gather_kernel(
    dp_size, clean, noise, aux, w_qkv, w_out, mixed_all, rate_all, qkv_all, out_all,
    mixed, rate, w_send, w_recv, t_send, t_recv, own_sem,
):
    dp_here, tensor_here, sibling, opposite, diagonal = places()
    part = clean.shape[0]
    qkv_rows = w_qkv.shape[0]
    peers = [(lax.rem(dp_here + step, dp_size), tensor_here) for step in range(1, dp_size)]
    greet(peers + [(dp_here, sibling), (dp_here, opposite)])
    weight_copies = []
    for which, (held, full) in enumerate(((w_qkv, qkv_all), (w_out, out_all))):
        for step, peer in enumerate(peers):
            copy = remote(
                held, rows_of(full, dp_here, qkv_rows), w_send.at[which, step], w_recv.at[which, step], peer
            )
            copy.start()
            weight_copies.append(copy)
    local_copies = [
        pltpu.make_async_copy(w_qkv, rows_of(qkv_all, dp_here, qkv_rows), own_sem.at[0]),
        pltpu.make_async_copy(w_out, rows_of(out_all, dp_here, qkv_rows), own_sem.at[1]),
    ]
    for copy in local_copies:
        copy.start()
    cos_t, sin_t = aux[3:4, :], aux[4:5, :]
    scale_up, amp_rate, offset = aux[0:1, :], aux[1:2, :], aux[2:3, :]

    @pl.loop(0, part // 16)
    def _(index):
        rows = pl.ds(pl.multiple_of(index * 16, 16), 16)
        clean_wide = clean[rows, :].astype(jnp.float32)
        noise_wide = noise[rows, :].astype(jnp.float32)
        noisy = cos_t * clean_wide + sin_t * noise_wide
        velocity = cos_t * noise_wide - sin_t * clean_wide
        inverse = lax.rsqrt(jnp.mean(noisy * noisy, axis=-1, keepdims=True) + norm_eps)
        cross = jnp.mean(noisy * velocity, axis=-1, keepdims=True)
        normed = noisy * inverse
        normed_rate = velocity * inverse - noisy * (inverse * inverse * inverse * cross)
        mixed[rows, :] = (normed * scale_up + offset).astype(jnp.bfloat16)
        rate[rows, :] = (normed_rate * scale_up + normed * amp_rate).astype(jnp.bfloat16)

    sends, forwards = [], []
    for which, (held, full) in enumerate(((mixed, mixed_all), (rate, rate_all))):
        spot = rows_of(full, tensor_here, part)
        to_opposite = remote(held, spot, t_send.at[which, 0], t_recv.at[which, 0], (dp_here, opposite))
        to_opposite.start()
        to_sibling = remote(held, spot, t_send.at[which, 1], t_recv.at[which, 1], (dp_here, sibling))
        to_sibling.start()
        own = pltpu.make_async_copy(held, spot, own_sem.at[2 + which])
        own.start()
        local_copies.append(own)
        arrived = rows_of(full, opposite, part)
        forward = remote(arrived, arrived, t_send.at[which, 2], t_recv.at[which, 2], (dp_here, sibling))
        sends.append((to_opposite, to_sibling))
        forwards.append(forward)
    for (to_opposite, _), forward in zip(sends, forwards):
        to_opposite.wait_recv()
        forward.start()
    for (to_opposite, to_sibling), forward in zip(sends, forwards):
        to_opposite.wait_send()
        to_sibling.wait()
        forward.wait()
    for copy in weight_copies:
        copy.wait()
    for copy in local_copies:
        copy.wait()


def gather_all(dp_size, clean, noise, aux, w_qkv, w_out):
    part, width = clean.shape
    low = jnp.bfloat16
    return pl.pallas_call(
        functools.partial(gather_kernel, dp_size),
        out_shape=(
            jax.ShapeDtypeStruct((4 * part, width), low),
            jax.ShapeDtypeStruct((4 * part, width), low),
            jax.ShapeDtypeStruct((dp_size * w_qkv.shape[0], w_qkv.shape[1]), low),
            jax.ShapeDtypeStruct((dp_size * w_out.shape[0], w_out.shape[1]), low),
        ),
        in_specs=[VMEM] * 5,
        out_specs=(HBM,) * 4,
        scratch_shapes=[
            pltpu.VMEM((part, width), low),
            pltpu.VMEM((part, width), low),
            pltpu.SemaphoreType.DMA((2, dp_size)),
            pltpu.SemaphoreType.DMA((2, dp_size)),
            pltpu.SemaphoreType.DMA((2, 3)),
            pltpu.SemaphoreType.DMA((2, 3)),
            pltpu.SemaphoreType.DMA((4,)),
        ],
        compiler_params=pltpu.CompilerParams(
            collective_id=0, has_side_effects=True, vmem_limit_bytes=32 * 2**20
        ),
    )(clean, noise, aux, w_qkv, w_out)


PIECES = 4


def target_kernel(
    clean, noise, aux, partial, target_all, first, from_sibling, from_opposite, summed, target,
    load_sem, r_send, r_recv, g_send, g_recv,
):
    dp_here, tensor_here, sibling, opposite, diagonal = places()
    part = clean.shape[0]
    piece = part // PIECES
    greet([(dp_here, sibling), (dp_here, opposite)])

    def block(owner, index):
        return rows_of(partial, owner * PIECES + index, piece)

    def slot(ref, index):
        return ref.at[pl.ds(index * piece, piece)]

    cross, direct, across, loads = [], [], [], []
    for index in range(PIECES):
        copy = remote(
            block(diagonal, index), slot(from_sibling.at[0], index), r_send.at[0, index], r_recv.at[0, index],
            (dp_here, sibling),
        )
        copy.start()
        cross.append(copy)
        load = pltpu.make_async_copy(block(opposite, index), slot(first.at[0], index), load_sem.at[0, index])
        load.start()
        loads.append(load)
    own_loads = []
    for index in range(PIECES):
        copy = remote(
            block(sibling, index), slot(from_sibling.at[1], index), r_send.at[1, index], r_recv.at[1, index],
            (dp_here, sibling),
        )
        copy.start()
        direct.append(copy)
        load = pltpu.make_async_copy(block(tensor_here, index), slot(first.at[1], index), load_sem.at[1, index])
        load.start()
        own_loads.append(load)
    for index in range(PIECES):
        cross[index].wait_recv()
        loads[index].wait()
        rows = pl.ds(index * piece, piece)
        total = first[0, rows, :].astype(jnp.float32) + from_sibling[0, rows, :].astype(jnp.float32)
        summed[rows, :] = total.astype(jnp.bfloat16)
        copy = remote(
            slot(summed, index), slot(from_opposite, index), r_send.at[2, index], r_recv.at[2, index],
            (dp_here, opposite),
        )
        copy.start()
        across.append(copy)
    cos_t, sin_t = aux[3:4, :], aux[4:5, :]
    sends, forwards = [], []

    def spot(owner, index):
        return rows_of(target_all, owner * PIECES + index, piece)

    for index in range(PIECES):
        across[index].wait_recv()
        direct[index].wait_recv()
        own_loads[index].wait()
        rows = pl.ds(index * piece, piece)
        clean_wide = clean[rows, :].astype(jnp.float32)
        noise_wide = noise[rows, :].astype(jnp.float32)
        noisy = cos_t * clean_wide + sin_t * noise_wide
        velocity = cos_t * noise_wide - sin_t * clean_wide
        moved = (
            first[1, rows, :].astype(jnp.float32)
            + from_sibling[1, rows, :].astype(jnp.float32)
            + from_opposite[rows, :].astype(jnp.float32)
        )
        value = -(cos_t * cos_t) * (noisy - velocity) - cos_t * sin_t * (noisy + velocity) - moved
        target[rows, :] = value.astype(jnp.bfloat16)
        held = slot(target, index)
        to_opposite = remote(
            held, spot(tensor_here, index), g_send.at[0, index], g_recv.at[0, index], (dp_here, opposite)
        )
        to_opposite.start()
        to_sibling = remote(
            held, spot(tensor_here, index), g_send.at[1, index], g_recv.at[1, index], (dp_here, sibling)
        )
        to_sibling.start()
        own = pltpu.make_async_copy(held, spot(tensor_here, index), load_sem.at[2, index])
        own.start()
        forward = remote(
            spot(opposite, index), spot(opposite, index), g_send.at[2, index], g_recv.at[2, index], (dp_here, sibling)
        )
        sends.append((to_opposite, to_sibling, own, forward))
    for to_opposite, to_sibling, own, forward in sends:
        to_opposite.wait_recv()
        forward.start()
    for index, (to_opposite, to_sibling, own, forward) in enumerate(sends):
        to_opposite.wait_send()
        to_sibling.wait()
        own.wait()
        forward.wait()
        cross[index].wait_send()
        direct[index].wait_send()
        across[index].wait_send()


def gather_target(clean, noise, aux, partial):
    part, width = clean.shape
    low = jnp.bfloat16
    return pl.pallas_call(
        target_kernel,
        out_shape=jax.ShapeDtypeStruct((4 * part, width), low),
        in_specs=[VMEM, VMEM, VMEM, HBM],
        out_specs=HBM,
        scratch_shapes=[
            pltpu.VMEM((2, part, width), low),
            pltpu.VMEM((2, part, width), low),
            pltpu.VMEM((part, width), low),
            pltpu.VMEM((part, width), low),
            pltpu.VMEM((part, width), low),
            pltpu.SemaphoreType.DMA((3, PIECES)),
            pltpu.SemaphoreType.DMA((3, PIECES)),
            pltpu.SemaphoreType.DMA((3, PIECES)),
            pltpu.SemaphoreType.DMA((3, PIECES)),
            pltpu.SemaphoreType.DMA((3, PIECES)),
        ],
        compiler_params=pltpu.CompilerParams(
            collective_id=1, has_side_effects=True, vmem_limit_bytes=32 * 2**20
        ),
    )(clean, noise, aux, partial)


def scatter_kernel(
    dp_size, in_partial, out_partial, in_sum, out_sum, in_slots, out_slots, send_sem, recv_sem, own_sem
):
    dp_here, tensor_here, _, _, _ = places()
    rows = in_sum.shape[0]
    peers = [(lax.rem(dp_here + step, dp_size), tensor_here) for step in range(1, dp_size)]
    greet(peers)
    pairs = ((in_partial, in_slots, in_sum), (out_partial, out_slots, out_sum))
    copies, own_copies = [], []
    for which, (source, slots, _) in enumerate(pairs):
        row = []
        for step, peer in enumerate(peers):
            copy = remote(
                rows_of(source, peer[0], rows), slots.at[step + 1], send_sem.at[which, step],
                recv_sem.at[which, step], peer,
            )
            copy.start()
            row.append(copy)
        copies.append(row)
        own = pltpu.make_async_copy(rows_of(source, dp_here, rows), slots.at[0], own_sem.at[which])
        own.start()
        own_copies.append(own)
    tile = min(rows, 32)
    for which, (_, slots, total) in enumerate(pairs):
        own_copies[which].wait()
        for copy in copies[which]:
            copy.wait_recv()

        @pl.loop(0, rows // tile)
        def _(index):
            spot = pl.ds(pl.multiple_of(index * tile, tile), tile)
            value = slots[0, spot, :].astype(jnp.float32)
            value = lax.fori_loop(
                1, dp_size, lambda step, held: held + slots[step, spot, :].astype(jnp.float32), value
            )
            total[spot, :] = value

    for row in copies:
        for copy in row:
            copy.wait_send()


def scatter_all(dp_size, in_partial, out_partial):
    rows = in_partial.shape[0] // dp_size
    in_cols, out_cols = in_partial.shape[1], out_partial.shape[1]
    low = jnp.bfloat16
    return pl.pallas_call(
        functools.partial(scatter_kernel, dp_size),
        out_shape=(
            jax.ShapeDtypeStruct((rows, in_cols), jnp.float32),
            jax.ShapeDtypeStruct((rows, out_cols), jnp.float32),
        ),
        in_specs=[HBM, HBM],
        out_specs=(VMEM, VMEM),
        scratch_shapes=[
            pltpu.VMEM((dp_size, rows, in_cols), low),
            pltpu.VMEM((dp_size, rows, out_cols), low),
            pltpu.SemaphoreType.DMA((2, dp_size)),
            pltpu.SemaphoreType.DMA((2, dp_size)),
            pltpu.SemaphoreType.DMA((2,)),
        ],
        compiler_params=pltpu.CompilerParams(
            collective_id=2, has_side_effects=True, vmem_limit_bytes=32 * 2**20
        ),
    )(in_partial, out_partial)


def local(dp_size, clean_latents, noise_latents, step_index, labels, class_shift, w_qkv, w_out_t):
    latent_count, part_len, model_width = clean_latents.shape
    head_cols = w_out_t.shape[1]
    heads_here = head_cols // HEAD_DIM
    score_scale = 1.0 / math.sqrt(HEAD_DIM)
    seq_len = part_len * 4
    loss_scale = 1.0 / math.sqrt(dp_size * latent_count * seq_len)
    step_times, amplitude, amp_rate = time_terms(step_index, model_width)
    offset = lax.dynamic_slice(class_shift, (labels[0], 0), (1, model_width)).astype(jnp.float32)
    cos_t, sin_t = jnp.cos(step_times[0]), jnp.sin(step_times[0])
    row = (1, model_width)
    aux = jnp.concatenate(
        [
            1.0 + amplitude,
            amp_rate,
            offset,
            jnp.broadcast_to(cos_t, row),
            jnp.broadcast_to(sin_t, row),
            jnp.zeros((3, model_width), jnp.float32),
        ]
    )
    clean, noise = clean_latents[0], noise_latents[0]
    mixed_rows, rate_rows, qkv_all, out_all = gather_all(dp_size, clean, noise, aux, w_qkv, w_out_t)
    heads_shape = (1, seq_len, heads_here, 3, HEAD_DIM)
    projected = jnp.dot(mixed_rows, qkv_all, preferred_element_type=jnp.float32)
    projected_rate = jnp.dot(rate_rows, qkv_all, preferred_element_type=jnp.float32)
    projected = projected.astype(jnp.bfloat16).reshape(heads_shape)
    projected_rate = projected_rate.astype(jnp.bfloat16).reshape(heads_shape)
    attn_probs, probs_low, attn_out, attn_rate = attend(projected, projected_rate, score_scale)
    attn_rows = attn_out.astype(jnp.bfloat16).reshape(seq_len, head_cols)
    blend = (cos_t * cos_t * attn_out + cos_t * sin_t * attn_rate).astype(jnp.bfloat16)
    partial = lax.dot_general(
        blend.reshape(seq_len, head_cols), out_all, (((1,), (1,)), ((), ())),
        preferred_element_type=jnp.float32,
    ).astype(jnp.bfloat16)
    target = gather_target(clean, noise, aux, partial)
    target_wide = target.astype(jnp.float32)
    spread = jnp.sqrt(jnp.sum(target_wide * target_wide) / (seq_len * model_width))
    scale = -loss_scale / (spread + target_floor)
    out_partial = (row_contract(target, attn_rows) * scale).astype(jnp.bfloat16)
    attn_grad = jnp.dot(target, out_all, preferred_element_type=jnp.float32) * scale
    attn_grad = attn_grad.astype(jnp.bfloat16).reshape(1, seq_len, heads_here, HEAD_DIM)
    qkv_grad = attend_back(attn_grad, attn_probs, probs_low, projected, score_scale)
    in_partial = row_contract(mixed_rows, qkv_grad.reshape(seq_len, 3 * head_cols))
    return scatter_all(dp_size, in_partial.astype(jnp.bfloat16), out_partial)


def solution(mesh):
    in_specs = (
        P("dp", "tensor", None),
        P("dp", "tensor", None),
        P("dp"),
        P("dp"),
        P(),
        P("dp", "tensor"),
        P("dp", "tensor"),
    )
    out_specs = (P("dp", "tensor"), P("dp", "tensor"))
    step = functools.partial(local, mesh.shape["dp"])
    return jax.shard_map(step, mesh=mesh, in_specs=in_specs, out_specs=out_specs, check_vma=False)
```

time: 473 us -> 270 us (0.57)
  the two profiles are of different devices: /device:TPU:0 before, /device:TPU:13 now
where the time goes in v1:
time: 270 us
  Pallas kernels  219 us (81%)
  matrix products  37 us (14%)
  local copies, waits for them, and re-layouts  8.14 us (3%)
  between operations  3.03 us (1%)
  other arithmetic  2.82 us (1%)
    pallas_call x1, Pallas kernels, gather_all(): pl.pallas_call(functools.partial(gather_kernel, dp_size), out_shape=(jax....  95.1 us
    pallas_call x1, Pallas kernels, scatter_all(): pl.pallas_call(functools.partial(scatter_kernel, dp_size), out_shape=(jax...  95 us
    pallas_call x1, Pallas kernels, gather_target(): pl.pallas_call(target_kernel, out_shape=jax.ShapeDtypeStruct((4 * part, w...  28.6 us
    dot_general x9, matrix products, low_einsum(): jnp.einsum(form, left_part, right_part, preferred_element_type=jnp.float32)  26.1 us
    unnamed x22, local copies, waits for them, and re-layouts  7.42 us

profile of v1, /device:TPU:13, one launch (start us, length us, event | category | flops | bytes accessed | tf_op | source)
XLA Modules:
  0.0 269.7 jit_solution(9485232207020372631)
XLA Ops:
  2.1 0.8 dynamic-slice_convert_fusion
  2.9 0.3 cosine_multiply_fusion
  3.3 1.0 copy-done
  4.3 1.0 copy-done.2
  5.4 1.0 copy-done.4
  6.3 0.9 copy-done.5
  7.3 95.1 %shard_map.86 = (bf16[512,2048]{1,0:T(8,128)(2,1)S(1)}, bf16[512,2048]{1,0:T(8,128)(2,1)S(1)}, bf16[2048,768]{1,0:T(8,128)(2,1)S(1)}, bf16[2048,256]{1,0:T(8,128)(2,1)S(1)}) custom-call(bf16[128,2048]{1,0:T(8,128)(2,1)S(1)} %bitcast.147, bf16[128,2048]{1,0:T(8,128)(2,1)S(1)} %bitcast.149, f32[8,2048]{1,0:T(8,128)S(1)} %concatenate.6.aux, ...), custom_call_target="tpu_custom_call" | custom-call | tf_op jit(solution)/shard_map/pallas_call | solution.py:181
  102.4 1.8 convolution_convert_fusion.2
  104.2 1.8 convolution_convert_fusion.3
  106.0 0.3 copy.25
  106.3 0.3 copy.30
  106.5 1.8 fusion.35
  108.3 2.2 fusion.63
  110.5 4.1 %multiply_reduce_fusion.2 = (f32[2,512]{1,0:T(2,128)S(1)}, f32[2,512,512]{1,2,0:T(8,128)}) fusion(f32[2,512,512]{1,2,0:T(8,128)} %get-tuple-element.11, f32[2,512]{1,0:T(2,128)S(1)} %get-tuple-element.10, f32[2,512,512]{1,2,0:T(8,128)} %fusion.35, bf16[1,512,2,3,128]{1,4,3,2,0:T(8,128)(2,1)S(1)} %bitcast.162, bf16[1,512,2,3,128]{1,4,3,2,0:T(8,128)(2,1)S(1)} %bitcast.153), kind=kOutput, calls=%fused_computation.11 | convolution fusion | flops 136838144 | bytes 6823936 | tf_op jit(solution)/shard_map/lqhd,lkhd->lhqk/dot_general | solution.py:28
  114.6 3.0 %fusion.30 = f32[2,128,512]{2,1,0:T(8,128)S(1)} fusion(f32[2,512,512]{1,2,0:T(8,128)} %get-tuple-element.13, f32[2,512]{1,0:T(2,128)S(1)} %get-tuple-element.12, bf16[1,512,2,3,128]{1,4,3,2,0:T(8,128)(2,1)S(1)} %bitcast.154, f32[2,512]{1,0:T(2,128)S(1)} %get-tuple-element.10), kind=kOutput, calls=%fused_computation.32 | convolution fusion | flops 271582720 | bytes 3416064 | tf_op jit(solution)/shard_map/lhqk,lkhd->lqhd/dot_general | solution.py:28
  117.6 2.1 fusion.64
  119.6 2.2 fusion.22
  121.9 0.8 convolution_convert_fusion.1.partial
  122.6 0.3 copy-done.1
  123.1 28.6 %shard_map.87 = bf16[512,2048]{1,0:T(8,128)(2,1)S(1)} custom-call(bf16[128,2048]{1,0:T(8,128)(2,1)S(1)} %bitcast.148, bf16[128,2048]{1,0:T(8,128)(2,1)S(1)} %bitcast.150, f32[8,2048]{1,0:T(8,128)S(1)} %concatenate.6.aux, bf16[512,2048]{1,0:T(8,128)(2,1)S(1)} %convolution_convert_fusion.1.partial), custom_call_target="tpu_custom_call" | custom-call | tf_op jit(solution)/shard_map/pallas_call | solution.py:311
  151.7 1.7 multiply_reduce_fusion
  154.0 0.8 fusion.15
  154.8 1.7 fusion.2.out_partial
  156.6 2.3 fusion.29
  158.9 1.8 fusion.37
  160.7 4.5 %fusion.26 = bf16[1,512,2,1,128]{1,4,2,3,0:T(8,128)(2,1)S(1)} fusion(f32[2,512,512]{1,2,0:T(8,128)} %fusion.37, bf16[1,512,2,3,128]{1,4,3,2,0:T(8,128)(2,1)S(1)} %bitcast.159, f32[2,512,512]{1,2,0:T(8,128)} %get-tuple-element.11, f32[2,512]{1,0:T(2,128)S(1)} %get-tuple-element.10), kind=kOutput, calls=%fused_computation.30 | convolution fusion | flops 138020352 | bytes 8921088 | tf_op jit(solution)/shard_map/lhqk,lkhd->lqhd/dot_general | solution.py:28
  165.2 4.4 %fusion.23 = bf16[1,512,2,1,128]{1,4,2,3,0:T(8,128)(2,1)S(1)} fusion(f32[2,512,512]{1,2,0:T(8,128)} %fusion.37, bf16[1,512,2,3,128]{1,4,3,2,0:T(8,128)(2,1)S(1)} %bitcast.160, f32[2,512,512]{1,2,0:T(8,128)} %get-tuple-element.11, f32[2,512]{1,0:T(2,128)S(1)} %get-tuple-element.10), kind=kOutput, calls=%fused_computation.29 | convolution fusion | flops 138020352 | bytes 8921088 | tf_op jit(solution)/shard_map/lhqk,lqhd->lkhd/dot_general | solution.py:28
  169.8 1.4 copy-done.7
  171.2 1.9 convolution_convert_fusion.in_partial
  173.1 95.0 %shard_map.88 = (f32[256,768]{1,0:T(8,128)S(1)}, f32[256,256]{1,0:T(8,128)S(1)}) custom-call(bf16[2048,768]{1,0:T(8,128)(2,1)S(1)} %convolution_convert_fusion.in_partial, bf16[2048,256]{1,0:T(8,128)(2,1)S(1)} %fusion.2.out_partial), custom_call_target="tpu_custom_call" | custom-call | tf_op jit(solution)/shard_map/pallas_call | solution.py:380
  268.1 0.9 copy.64
  269.0 0.7 copy.65
  (20 shorter events, 0.4 us)
Async XLA Ops:
  3.3 1.0 copy-start
  4.3 1.0 copy-start.2
  5.3 1.0 copy-start.4
  6.3 0.9 copy-start.5
  102.4 1.8 copy-start.6
  106.2 13.4 %copy-start.8 = (bf16[512,768]{0,1:T(8,128)(2,1)}, bf16[512,768]{0,1:T(8,128)(2,1)S(1)}, u32[]{:S(2)}) copy-start(bf16[512,768]{0,1:T(8,128)(2,1)S(1)} %copy.25) | copy-start | bytes 2359300
  121.8 1.0 copy-start.1
  121.9 1.2 copy-start.3
  156.5 2.4 copy-start.9
  169.6 1.6 copy-start.7

commit v2 on v1

--- a/solution.py
+++ b/solution.py
@@ -110,21 +110,40 @@
 
 def gather_kernel(
     dp_size, clean, noise, aux, w_qkv, w_out, mixed_all, rate_all, qkv_all, out_all,
-    mixed, rate, w_send, w_recv, t_send, t_recv, own_sem,
+    mixed, rate, w_send, w_recv, p_send, p_recv, t_send, t_recv, own_sem,
 ):
     dp_here, tensor_here, sibling, opposite, diagonal = places()
     part = clean.shape[0]
     qkv_rows = w_qkv.shape[0]
-    peers = [(lax.rem(dp_here + step, dp_size), tensor_here) for step in range(1, dp_size)]
-    greet(peers + [(dp_here, sibling), (dp_here, opposite)])
-    weight_copies = []
-    for which, (held, full) in enumerate(((w_qkv, qkv_all), (w_out, out_all))):
-        for step, peer in enumerate(peers):
-            copy = remote(
-                held, rows_of(full, dp_here, qkv_rows), w_send.at[which, step], w_recv.at[which, step], peer
-            )
-            copy.start()
-            weight_copies.append(copy)
+    outer = dp_size // 2
+    outer_here, pair_here = dp_here // 2, lax.rem(dp_here, 2)
+    onward = (lax.rem(outer_here + 1, outer) * 2 + pair_here, tensor_here)
+    backward = (lax.rem(outer_here + outer - 1, outer) * 2 + pair_here, tensor_here)
+    partner = (outer_here * 2 + 1 - pair_here, tensor_here)
+    greet([onward, backward, partner, (dp_here, sibling), (dp_here, opposite)])
+    pieces = min(2, qkv_rows // 16)
+    piece = qkv_rows // pieces
+    ring_copies, pair_copies = {}, []
+
+    def ring_step(step):
+        block = lax.rem(outer_here - step + outer, outer) * 2 + pair_here
+        for which, (held, full) in enumerate(((w_qkv, qkv_all), (w_out, out_all))):
+            for index in range(pieces):
+                spot = rows_of(full, block * pieces + index, piece)
+                source = held.at[pl.ds(index * piece, piece)] if step == 0 else spot
+                if step > 0:
+                    ring_copies[step - 1, which, index].wait_recv()
+                if step < outer - 1:
+                    copy = remote(
+                        source, spot, w_send.at[step, which, index], w_recv.at[step, which, index], onward
+                    )
+                    copy.start()
+                    ring_copies[step, which, index] = copy
+                copy = remote(source, spot, p_send.at[step, which, index], p_recv.at[step, which, index], partner)
+                copy.start()
+                pair_copies.append(copy)
+
+    ring_step(0)
     local_copies = [
         pltpu.make_async_copy(w_qkv, rows_of(qkv_all, dp_here, qkv_rows), own_sem.at[0]),
         pltpu.make_async_copy(w_out, rows_of(out_all, dp_here, qkv_rows), own_sem.at[1]),
@@ -162,14 +181,19 @@
         forward = remote(arrived, arrived, t_send.at[which, 2], t_recv.at[which, 2], (dp_here, sibling))
         sends.append((to_opposite, to_sibling))
         forwards.append(forward)
-    for (to_opposite, _), forward in zip(sends, forwards):
-        to_opposite.wait_recv()
-        forward.start()
+    for step in range(max(outer - 1, 2)):
+        if step + 1 < outer:
+            ring_step(step + 1)
+        if step < 2:
+            sends[step][0].wait_recv()
+            forwards[step].start()
     for (to_opposite, to_sibling), forward in zip(sends, forwards):
         to_opposite.wait_send()
         to_sibling.wait()
         forward.wait()
-    for copy in weight_copies:
+    for copy in ring_copies.values():
+        copy.wait_send()
+    for copy in pair_copies:
         copy.wait()
     for copy in local_copies:
         copy.wait()
@@ -191,8 +215,10 @@
         scratch_shapes=[
             pltpu.VMEM((part, width), low),
             pltpu.VMEM((part, width), low),
-            pltpu.SemaphoreType.DMA((2, dp_size)),
-            pltpu.SemaphoreType.DMA((2, dp_size)),
+            pltpu.SemaphoreType.DMA((dp_size // 2, 2, 2)),
+            pltpu.SemaphoreType.DMA((dp_size // 2, 2, 2)),
+            pltpu.SemaphoreType.DMA((dp_size // 2, 2, 2)),
+            pltpu.SemaphoreType.DMA((dp_size // 2, 2, 2)),
             pltpu.SemaphoreType.DMA((2, 3)),
             pltpu.SemaphoreType.DMA((2, 3)),
             pltpu.SemaphoreType.DMA((4,)),
@@ -332,51 +358,71 @@
 
 
 def scatter_kernel(
-    dp_size, in_partial, out_partial, in_sum, out_sum, in_slots, out_slots, send_sem, recv_sem, own_sem
+    dp_size, in_partial, out_partial, in_sum, out_sum, in_own, out_own, in_pair, out_pair, in_ring, out_ring,
+    in_sent, out_sent, p_send, p_recv, r_send, r_recv, own_sem,
 ):
     dp_here, tensor_here, _, _, _ = places()
     rows = in_sum.shape[0]
-    peers = [(lax.rem(dp_here + step, dp_size), tensor_here) for step in range(1, dp_size)]
-    greet(peers)
-    pairs = ((in_partial, in_slots, in_sum), (out_partial, out_slots, out_sum))
-    copies, own_copies = [], []
-    for which, (source, slots, _) in enumerate(pairs):
-        row = []
-        for step, peer in enumerate(peers):
-            copy = remote(
-                rows_of(source, peer[0], rows), slots.at[step + 1], send_sem.at[which, step],
-                recv_sem.at[which, step], peer,
+    outer = dp_size // 2
+    outer_here, pair_here = dp_here // 2, lax.rem(dp_here, 2)
+    onward = (lax.rem(outer_here + 1, outer) * 2 + pair_here, tensor_here)
+    backward = (lax.rem(outer_here + outer - 1, outer) * 2 + pair_here, tensor_here)
+    partner = (outer_here * 2 + 1 - pair_here, tensor_here)
+    greet([onward, backward, partner])
+    pieces = min(4, rows // 16)
+    piece = rows // pieces
+    arrays = (
+        (out_partial, out_own, out_pair, out_ring, out_sent, out_sum),
+        (in_partial, in_own, in_pair, in_ring, in_sent, in_sum),
+    )
+    loads, pair_copies, ring_copies = {}, {}, {}
+    for step in range(outer):
+        block = lax.rem(outer_here - step - 1 + outer, outer) * 2
+        for which, (partial, own, pair, _, _, _) in enumerate(arrays):
+            for index in range(pieces):
+                copy = remote(
+                    rows_of(partial, (block + 1 - pair_here) * pieces + index, piece),
+                    pair.at[step, pl.ds(index * piece, piece)],
+                    p_send.at[step, which, index], p_recv.at[step, which, index], partner,
+                )
+                copy.start()
+                pair_copies[step, which, index] = copy
+            load = pltpu.make_async_copy(
+                rows_of(partial, block + pair_here, rows), own.at[step], own_sem.at[step, which]
             )
-            copy.start()
-            row.append(copy)
-        copies.append(row)
-        own = pltpu.make_async_copy(rows_of(source, dp_here, rows), slots.at[0], own_sem.at[which])
-        own.start()
-        own_copies.append(own)
-    tile = min(rows, 32)
-    for which, (_, slots, total) in enumerate(pairs):
-        own_copies[which].wait()
-        for copy in copies[which]:
-            copy.wait_recv()
-
-        @pl.loop(0, rows // tile)
-        def _(index):
-            spot = pl.ds(pl.multiple_of(index * tile, tile), tile)
-            value = slots[0, spot, :].astype(jnp.float32)
-            value = lax.fori_loop(
-                1, dp_size, lambda step, held: held + slots[step, spot, :].astype(jnp.float32), value
-            )
-            total[spot, :] = value
-
-    for row in copies:
-        for copy in row:
-            copy.wait_send()
+            load.start()
+            loads[step, which] = load
+    for step in range(outer):
+        for which, (_, own, pair, ring, sent, total) in enumerate(arrays):
+            loads[step, which].wait()
+            for index in range(pieces):
+                spot = pl.ds(index * piece, piece)
+                pair_copies[step, which, index].wait_recv()
+                value = own[step, spot, :].astype(jnp.float32) + pair[step, spot, :].astype(jnp.float32)
+                if step > 0:
+                    ring_copies[step - 1, which, index].wait_recv()
+                    value = value + ring[step - 1, spot, :].astype(jnp.float32)
+                if step == outer - 1:
+                    total[spot, :] = value
+                    continue
+                sent[step, spot, :] = value.astype(jnp.bfloat16)
+                copy = remote(
+                    sent.at[step, spot], ring.at[step, spot],
+                    r_send.at[step, which, index], r_recv.at[step, which, index], onward,
+                )
+                copy.start()
+                ring_copies[step, which, index] = copy
+    for copy in pair_copies.values():
+        copy.wait_send()
+    for copy in ring_copies.values():
+        copy.wait_send()
 
 
 def scatter_all(dp_size, in_partial, out_partial):
     rows = in_partial.shape[0] // dp_size
     in_cols, out_cols = in_partial.shape[1], out_partial.shape[1]
     low = jnp.bfloat16
+    outer = dp_size // 2
     return pl.pallas_call(
         functools.partial(scatter_kernel, dp_size),
         out_shape=(
@@ -385,13 +431,9 @@
         ),
         in_specs=[HBM, HBM],
         out_specs=(VMEM, VMEM),
-        scratch_shapes=[
-            pltpu.VMEM((dp_size, rows, in_cols), low),
-            pltpu.VMEM((dp_size, rows, out_cols), low),
-            pltpu.SemaphoreType.DMA((2, dp_size)),
-            pltpu.SemaphoreType.DMA((2, dp_size)),
-            pltpu.SemaphoreType.DMA((2,)),
-        ],
+        scratch_shapes=[pltpu.VMEM((outer, rows, cols), low) for _ in range(4) for cols in (in_cols, out_cols)]
+        + [pltpu.SemaphoreType.DMA((outer, 2, 4)) for _ in range(4)]
+        + [pltpu.SemaphoreType.DMA((outer, 2))],
         compiler_params=pltpu.CompilerParams(
             collective_id=2, has_side_effects=True, vmem_limit_bytes=32 * 2**20
         ),

time: 270 us -> 182 us (0.67)
  the two profiles are of different devices: /device:TPU:13 before, /device:TPU:0 now
where the time goes in v2:
time: 182 us; the launch traced here: 181 us
  Pallas kernels  130 us (71%)
  matrix products  37 us (20%)
  local copies, waits for them, and re-layouts  8.14 us (4%)
  between operations  3.03 us (2%)
  other arithmetic  2.82 us (2%)
    pallas_call x1, Pallas kernels, gather_all(): pl.pallas_call(functools.partial(gather_kernel, dp_size), out_shape=(jax....  52.7 us
    pallas_call x1, Pallas kernels, scatter_all(): pl.pallas_call(functools.partial(scatter_kernel, dp_size), out_shape=(jax...  49.3 us
    pallas_call x1, Pallas kernels, gather_target(): pl.pallas_call(target_kernel, out_shape=jax.ShapeDtypeStruct((4 * part, w...  28.3 us
    dot_general x9, matrix products, low_einsum(): jnp.einsum(form, left_part, right_part, preferred_element_type=jnp.float32)  26.1 us
    unnamed x22, local copies, waits for them, and re-layouts  7.42 us

profile of v2, /device:TPU:0, one launch (start us, length us, event | category | flops | bytes accessed | tf_op | source)
XLA Modules:
  0.0 181.1 jit_solution(10636866042040258307)
XLA Ops:
  2.1 0.8 dynamic-slice_convert_fusion
  2.9 0.3 cosine_multiply_fusion
  3.3 1.0 copy-done
  4.3 1.0 copy-done.2
  5.4 1.0 copy-done.4
  6.3 0.9 copy-done.5
  7.3 52.7 %shard_map.86 = (bf16[512,2048]{1,0:T(8,128)(2,1)S(1)}, bf16[512,2048]{1,0:T(8,128)(2,1)S(1)}, bf16[2048,768]{1,0:T(8,128)(2,1)S(1)}, bf16[2048,256]{1,0:T(8,128)(2,1)S(1)}) custom-call(bf16[128,2048]{1,0:T(8,128)(2,1)S(1)} %bitcast.147, bf16[128,2048]{1,0:T(8,128)(2,1)S(1)} %bitcast.149, f32[8,2048]{1,0:T(8,128)S(1)} %concatenate.6.aux, ...), custom_call_target="tpu_custom_call" | custom-call | tf_op jit(solution)/shard_map/pallas_call | solution.py:205
  59.9 1.8 convolution_convert_fusion.2
  61.7 1.8 convolution_convert_fusion.3
  63.5 0.3 copy.25
  63.8 0.3 copy.30
  64.1 1.8 %fusion.35 = f32[2,512,512]{1,2,0:T(8,128)} fusion(bf16[1,512,2,3,128]{1,4,3,2,0:T(8,128)(2,1)S(1)} %bitcast.161, bf16[1,512,2,3,128]{1,4,3,2,0:T(8,128)(2,1)S(1)} %bitcast.151), kind=kOutput, calls=%fused_computation.42 | convolution fusion | flops 134217728 | bytes 2621440 | tf_op jit(solution)/shard_map/lqhd,lkhd->lhqk/dot_general | solution.py:28
  65.9 2.2 %fusion.63 = (f32[2,512]{1,0:T(2,128)S(1)}, f32[2,512,512]{1,2,0:T(8,128)}) fusion(bf16[1,512,2,3,128]{1,4,3,2,0:T(8,128)(2,1)S(1)} %bitcast.152), kind=kOutput, calls=%fused_computation.62 | convolution fusion | flops 135791104 | bytes 2625536 | tf_op jit(solution)/shard_map/sub | solution.py:43
  68.1 4.1 %multiply_reduce_fusion.2 = (f32[2,512]{1,0:T(2,128)S(1)}, f32[2,512,512]{1,2,0:T(8,128)}) fusion(f32[2,512,512]{1,2,0:T(8,128)} %get-tuple-element.11, f32[2,512]{1,0:T(2,128)S(1)} %get-tuple-element.10, f32[2,512,512]{1,2,0:T(8,128)} %fusion.35, bf16[1,512,2,3,128]{1,4,3,2,0:T(8,128)(2,1)S(1)} %bitcast.162, bf16[1,512,2,3,128]{1,4,3,2,0:T(8,128)(2,1)S(1)} %bitcast.153), kind=kOutput, calls=%fused_computation.11 | convolution fusion | flops 136838144 | bytes 6823936 | tf_op jit(solution)/shard_map/lqhd,lkhd->lhqk/dot_general | solution.py:28
  72.2 3.0 %fusion.30 = f32[2,128,512]{2,1,0:T(8,128)S(1)} fusion(f32[2,512,512]{1,2,0:T(8,128)} %get-tuple-element.13, f32[2,512]{1,0:T(2,128)S(1)} %get-tuple-element.12, bf16[1,512,2,3,128]{1,4,3,2,0:T(8,128)(2,1)S(1)} %bitcast.154, f32[2,512]{1,0:T(2,128)S(1)} %get-tuple-element.10), kind=kOutput, calls=%fused_computation.32 | convolution fusion | flops 271582720 | bytes 3416064 | tf_op jit(solution)/shard_map/lhqk,lkhd->lqhd/dot_general | solution.py:28
  75.2 2.1 %fusion.64 = (bf16[2,128,512]{2,1,0:T(8,128)(2,1)}, f32[2,128,512]{2,1,0:T(8,128)}) fusion(f32[2,512]{1,0:T(2,128)S(1)} %get-tuple-element.10, bf16[1,512,2,3,128]{1,4,3,2,0:T(8,128)(2,1)S(1)} %bitcast.155), kind=kOutput, calls=%fused_computation.63 | convolution fusion | flops 270665216 | bytes 1576960 | tf_op jit(solution)/shard_map/lhqk,lkhd->lqhd/dot_general | solution.py:28
  77.2 2.2 %fusion.22 = bf16[2,128,512]{2,1,0:T(8,128)(2,1)S(1)} fusion(f32[2,128,512]{2,1,0:T(8,128)S(1)} %fusion.30, f32[2,128,512]{2,1,0:T(8,128)} %get-tuple-element.15, bf16[1,512,2,3,128]{1,4,3,2,0:T(8,128)(2,1)S(1)} %bitcast.163, f32[]{:T(128)S(6)} %mul.135, f32[]{:T(128)S(6)} %mul.132, f32[2,512]{1,0:T(2,128)S(1)} %get-tuple-element.10, ...), kind=kOutput, calls=%fused_computation.28 | convolution fusion | flops 271189504 | bytes 2101256 | tf_op jit(solution)/shard_map/lhqk,lkhd->lqhd/dot_general | solution.py:28
  79.4 0.8 convolution_convert_fusion.1.partial
  80.2 0.3 copy-done.1
  80.6 28.3 %shard_map.87 = bf16[512,2048]{1,0:T(8,128)(2,1)S(1)} custom-call(bf16[128,2048]{1,0:T(8,128)(2,1)S(1)} %bitcast.148, bf16[128,2048]{1,0:T(8,128)(2,1)S(1)} %bitcast.150, f32[8,2048]{1,0:T(8,128)S(1)} %concatenate.6.aux, bf16[512,2048]{1,0:T(8,128)(2,1)S(1)} %convolution_convert_fusion.1.partial), custom_call_target="tpu_custom_call" | custom-call | tf_op jit(solution)/shard_map/pallas_call | solution.py:337
  108.9 1.7 multiply_reduce_fusion
  111.3 0.8 fusion.15
  112.0 1.7 fusion.2.out_partial
  113.8 2.3 %fusion.29 = bf16[1,512,2,1,128]{1,4,2,3,0:T(8,128)(2,1)S(1)} fusion(bf16[512,2,128]{0,2,1:T(8,128)(2,1)S(1)} %bitcast.165, f32[2,512]{1,0:T(2,128)S(1)} %get-tuple-element.10, bf16[1,512,2,3,128]{1,4,3,2,0:T(8,128)(2,1)} %bitcast.157), kind=kOutput, calls=%fused_computation.31 | convolution fusion | flops 270665216 | bytes 1052672 | tf_op jit(solution)/shard_map/lhqk,lqhd->lkhd/dot_general | solution.py:28
  116.1 1.8 %fusion.37 = f32[2,512,512]{1,2,0:T(8,128)} fusion(bf16[512,2,128]{0,2,1:T(8,128)(2,1)S(1)} %bitcast.166, bf16[1,512,2,3,128]{1,4,3,2,0:T(8,128)(2,1)S(1)} %bitcast.158), kind=kOutput, calls=%fused_computation.47 | convolution fusion | flops 134217728 | bytes 2621440 | tf_op jit(solution)/shard_map/lqhd,lkhd->lhqk/dot_general | solution.py:28
  117.9 4.5 %fusion.26 = bf16[1,512,2,1,128]{1,4,2,3,0:T(8,128)(2,1)S(1)} fusion(f32[2,512,512]{1,2,0:T(8,128)} %fusion.37, bf16[1,512,2,3,128]{1,4,3,2,0:T(8,128)(2,1)S(1)} %bitcast.159, f32[2,512,512]{1,2,0:T(8,128)} %get-tuple-element.11, f32[2,512]{1,0:T(2,128)S(1)} %get-tuple-element.10), kind=kOutput, calls=%fused_computation.30 | convolution fusion | flops 138020352 | bytes 8921088 | tf_op jit(solution)/shard_map/lhqk,lkhd->lqhd/dot_general | solution.py:28
  122.4 4.4 %fusion.23 = bf16[1,512,2,1,128]{1,4,2,3,0:T(8,128)(2,1)S(1)} fusion(f32[2,512,512]{1,2,0:T(8,128)} %fusion.37, bf16[1,512,2,3,128]{1,4,3,2,0:T(8,128)(2,1)S(1)} %bitcast.160, f32[2,512,512]{1,2,0:T(8,128)} %get-tuple-element.11, f32[2,512]{1,0:T(2,128)S(1)} %get-tuple-element.10), kind=kOutput, calls=%fused_computation.29 | convolution fusion | flops 138020352 | bytes 8921088 | tf_op jit(solution)/shard_map/lhqk,lqhd->lkhd/dot_general | solution.py:28
  127.0 1.4 copy-done.7
  128.4 1.9 %convolution_convert_fusion.in_partial = bf16[2048,768]{1,0:T(8,128)(2,1)S(1)} fusion(bf16[512,2048]{1,0:T(8,128)(2,1)S(1)} %copy-done.7, bf16[512,768]{0,1:T(8,128)(2,1)S(1)} %bitcast.164), kind=kOutput, calls=%fused_computation.3 | convolution fusion | flops 1612185600 | bytes 6029312 | tf_op jit(solution)/shard_map/dot_general | solution.py:71
  130.3 49.3 %shard_map.88 = (f32[256,768]{1,0:T(8,128)S(1)}, f32[256,256]{1,0:T(8,128)S(1)}) custom-call(bf16[2048,768]{1,0:T(8,128)(2,1)S(1)} %convolution_convert_fusion.in_partial, bf16[2048,256]{1,0:T(8,128)(2,1)S(1)} %fusion.2.out_partial), custom_call_target="tpu_custom_call" | custom-call | tf_op jit(solution)/shard_map/pallas_call | solution.py:426
  179.6 0.9 copy.64
  180.4 0.7 copy.65
  (20 shorter events, 0.4 us)
Async XLA Ops:
  3.3 1.0 copy-start
  4.3 1.0 copy-start.2
  5.3 1.0 copy-start.4
  6.3 0.9 copy-start.5
  59.9 1.8 copy-start.6
  63.8 13.4 %copy-start.8 = (bf16[512,768]{0,1:T(8,128)(2,1)}, bf16[512,768]{0,1:T(8,128)(2,1)S(1)}, u32[]{:S(2)}) copy-start(bf16[512,768]{0,1:T(8,128)(2,1)S(1)} %copy.25) | copy-start | bytes 2359300
  79.4 1.0 copy-start.1
  79.4 1.2 copy-start.3
  113.8 2.3 %copy-start.9 = (bf16[512,768]{0,1:T(8,128)(2,1)S(1)}, bf16[512,768]{0,1:T(8,128)(2,1)}, u32[]{:S(2)}) copy-start(bf16[512,768]{0,1:T(8,128)(2,1)} %copy-done.8) | copy-start | bytes 2359300
  126.8 1.6 copy-start.7

commit v3 on v2

--- a/solution.py
+++ b/solution.py
@@ -51,28 +51,6 @@
     return (attn_probs, probs_low, attn_out, attn_rate)
 
 
-def attend_back(attn_grad, attn_probs, probs_low, projected, score_scale):
-    query_part = projected[:, :, :, 0, :]
-    key_part = projected[:, :, :, 1, :]
-    value_part = projected[:, :, :, 2, :]
-    prob_grad = low_einsum("lqhd,lkhd->lhqk", attn_grad, value_part)
-    value_grad = low_einsum("lhqk,lqhd->lkhd", probs_low, attn_grad)
-    score_grad = (
-        attn_probs
-        * (prob_grad - jnp.sum(attn_probs * prob_grad, axis=-1, keepdims=True))
-        * score_scale
-    ).astype(jnp.bfloat16)
-    query_grad = low_einsum("lhqk,lkhd->lqhd", score_grad, key_part)
-    key_grad = low_einsum("lhqk,lqhd->lkhd", score_grad, query_part)
-    return jnp.stack([query_grad, key_grad, value_grad], axis=3).astype(jnp.bfloat16)
-
-
-def row_contract(left_part, right_part):
-    return lax.dot_general(
-        left_part, right_part, (((0,), (0,)), ((), ())), preferred_element_type=jnp.float32
-    )
-
-
 MESH = pl.DeviceIdType.MESH
 VMEM = pl.BlockSpec(memory_space=pltpu.VMEM)
 HBM = pl.BlockSpec(memory_space=pl.ANY)
@@ -110,11 +88,17 @@
 
 def gather_kernel(
     dp_size, clean, noise, aux, w_qkv, w_out, mixed_all, rate_all, qkv_all, out_all,
-    mixed, rate, w_send, w_recv, p_send, p_recv, t_send, t_recv, own_sem,
+    clean_held, noise_held, mixed, rate, w_send, w_recv, p_send, p_recv, t_send, t_recv, own_sem,
 ):
     dp_here, tensor_here, sibling, opposite, diagonal = places()
     part = clean.shape[0]
     qkv_rows = w_qkv.shape[0]
+    latent_loads = [
+        pltpu.make_async_copy(clean, clean_held, own_sem.at[4]),
+        pltpu.make_async_copy(noise, noise_held, own_sem.at[5]),
+    ]
+    for copy in latent_loads:
+        copy.start()
     outer = dp_size // 2
     outer_here, pair_here = dp_here // 2, lax.rem(dp_here, 2)
     onward = (lax.rem(outer_here + 1, outer) * 2 + pair_here, tensor_here)
@@ -150,14 +134,16 @@
     ]
     for copy in local_copies:
         copy.start()
+    for copy in latent_loads:
+        copy.wait()
     cos_t, sin_t = aux[3:4, :], aux[4:5, :]
     scale_up, amp_rate, offset = aux[0:1, :], aux[1:2, :], aux[2:3, :]
 
     @pl.loop(0, part // 16)
     def _(index):
         rows = pl.ds(pl.multiple_of(index * 16, 16), 16)
-        clean_wide = clean[rows, :].astype(jnp.float32)
-        noise_wide = noise[rows, :].astype(jnp.float32)
+        clean_wide = clean_held[rows, :].astype(jnp.float32)
+        noise_wide = noise_held[rows, :].astype(jnp.float32)
         noisy = cos_t * clean_wide + sin_t * noise_wide
         velocity = cos_t * noise_wide - sin_t * clean_wide
         inverse = lax.rsqrt(jnp.mean(noisy * noisy, axis=-1, keepdims=True) + norm_eps)
@@ -210,9 +196,11 @@
             jax.ShapeDtypeStruct((dp_size * w_qkv.shape[0], w_qkv.shape[1]), low),
             jax.ShapeDtypeStruct((dp_size * w_out.shape[0], w_out.shape[1]), low),
         ),
-        in_specs=[VMEM] * 5,
+        in_specs=[HBM, HBM, VMEM, HBM, HBM],
         out_specs=(HBM,) * 4,
         scratch_shapes=[
+            pltpu.VMEM((part, width), low),
+            pltpu.VMEM((part, width), low),
             pltpu.VMEM((part, width), low),
             pltpu.VMEM((part, width), low),
             pltpu.SemaphoreType.DMA((dp_size // 2, 2, 2)),
@@ -221,10 +209,10 @@
             pltpu.SemaphoreType.DMA((dp_size // 2, 2, 2)),
             pltpu.SemaphoreType.DMA((2, 3)),
             pltpu.SemaphoreType.DMA((2, 3)),
-            pltpu.SemaphoreType.DMA((4,)),
+            pltpu.SemaphoreType.DMA((6,)),
         ],
         compiler_params=pltpu.CompilerParams(
-            collective_id=0, has_side_effects=True, vmem_limit_bytes=32 * 2**20
+            collective_id=0, has_side_effects=True, vmem_limit_bytes=60 * 2**20
         ),
     )(clean, noise, aux, w_qkv, w_out)
 
@@ -357,12 +345,20 @@
     )(clean, noise, aux, partial)
 
 
-def scatter_kernel(
-    dp_size, in_partial, out_partial, in_sum, out_sum, in_own, out_own, in_pair, out_pair, in_ring, out_ring,
-    in_sent, out_sent, p_send, p_recv, r_send, r_recv, own_sem,
+def dot(left, right, left_dim, right_dim):
+    return lax.dot_general(
+        left, right, (((left_dim,), (right_dim,)), ((), ())), preferred_element_type=jnp.float32
+    )
+
+
+def back_kernel(
+    dp_size, loss_scale, score_scale, target, attn_rows, out_all, mixed, projected, probs, in_sum, out_sum,
+    in_full, out_full, in_low, out_low, in_pair, out_pair, in_ring, out_ring, in_sent, out_sent,
+    attn_grad, qkv_grad, p_send, p_recv, r_send, r_recv,
 ):
     dp_here, tensor_here, _, _, _ = places()
     rows = in_sum.shape[0]
+    seq_len, width = target.shape
     outer = dp_size // 2
     outer_here, pair_here = dp_here // 2, lax.rem(dp_here, 2)
     onward = (lax.rem(outer_here + 1, outer) * 2 + pair_here, tensor_here)
@@ -371,73 +367,146 @@
     greet([onward, backward, partner])
     pieces = min(4, rows // 16)
     piece = rows // pieces
-    arrays = (
-        (out_partial, out_own, out_pair, out_ring, out_sent, out_sum),
-        (in_partial, in_own, in_pair, in_ring, in_sent, in_sum),
-    )
-    loads, pair_copies, ring_copies = {}, {}, {}
+    out_set = (out_full, out_low, out_pair, out_ring, out_sent, out_sum)
+    in_set = (in_full, in_low, in_pair, in_ring, in_sent, in_sum)
+    pair_copies, ring_copies = {}, {}
+
+    def squares(index, held):
+        spot = pl.ds(pl.multiple_of(index * 16, 16), 16)
+        value = target[spot, :].astype(jnp.float32)
+        return held + value * value
+
+    total = lax.fori_loop(0, seq_len // 16, squares, jnp.zeros((16, width), jnp.float32))
+    total = jnp.sum(jnp.sum(total, axis=0, keepdims=True), axis=1, keepdims=True)
+    scale = -loss_scale / (jnp.sqrt(total / (seq_len * width)) + target_floor)
+
+    def out_chunk(spot):
+        return dot(target[:, spot], attn_rows[...], 0, 0) * scale
+
+    def in_chunk(spot):
+        return dot(mixed[:, spot], qkv_grad[...], 0, 0)
+
+    def block_of(step):
+        return lax.rem(outer_here - step - 1 + outer, outer) * 2
+
+    def send_pair(step, which, low, pair):
+        for index in range(pieces):
+            copy = remote(
+                rows_of(low, (block_of(step) + 1 - pair_here) * pieces + index, piece),
+                pair.at[step, pl.ds(index * piece, piece)],
+                p_send.at[step, which, index], p_recv.at[step, which, index], partner,
+            )
+            copy.start()
+            pair_copies[step, which, index] = copy
+
+    def make_all(which, chunk, arrays):
+        full, low, pair = arrays[:3]
+        if rows % 128 == 0:
+            for step in range(outer):
+                spot = pl.ds(pl.multiple_of((block_of(step) + 1 - pair_here) * rows, rows), rows)
+                low[spot, :] = chunk(spot).astype(jnp.bfloat16)
+                send_pair(step, which, low, pair)
+            for step in range(outer):
+                spot = pl.ds(pl.multiple_of((block_of(step) + pair_here) * rows, rows), rows)
+                full[spot, :] = chunk(spot)
+        else:
+
+            @pl.loop(0, width // 128)
+            def _(index):
+                spot = pl.ds(pl.multiple_of(index * 128, 128), 128)
+                value = chunk(spot)
+                full[spot, :] = value
+                low[spot, :] = value.astype(jnp.bfloat16)
+
+            for step in range(outer):
+                send_pair(step, which, low, pair)
+
+    def ring_step(step, which, arrays):
+        full, _, pair, ring, sent, total = arrays
+        for index in range(pieces):
+            spot = pl.ds(index * piece, piece)
+            own = pl.ds(pl.multiple_of((block_of(step) + pair_here) * rows + index * piece, piece), piece)
+            pair_copies[step, which, index].wait_recv()
+            value = full[own, :] + pair[step, spot, :].astype(jnp.float32)
+            if step > 0:
+                ring_copies[step - 1, which, index].wait_recv()
+                value = value + ring[step - 1, spot, :].astype(jnp.float32)
+            if step == outer - 1:
+                total[spot, :] = value
+                continue
+            sent[step, spot, :] = value.astype(jnp.bfloat16)
+            copy = remote(
+                sent.at[step, spot], ring.at[step, spot],
+                r_send.at[step, which, index], r_recv.at[step, which, index], onward,
+            )
+            copy.start()
+            ring_copies[step, which, index] = copy
+
+    make_all(0, out_chunk, out_set)
+    tile = min(256, seq_len)
+    for start in range(0, seq_len, tile):
+        spot = pl.ds(start, tile)
+        attn_grad[spot, :] = (dot(target[spot, :], out_all[...], 1, 0) * scale).astype(jnp.bfloat16)
+    ring_step(0, 0, out_set)
+    done = 1
+    for head in range(probs.shape[0]):
+        base = head * 3 * HEAD_DIM
+        query = projected[:, base : base + HEAD_DIM]
+        key = projected[:, base + HEAD_DIM : base + 2 * HEAD_DIM]
+        value = projected[:, base + 2 * HEAD_DIM : base + 3 * HEAD_DIM]
+        key_grad = jnp.zeros((seq_len, HEAD_DIM), jnp.float32)
+        value_grad = jnp.zeros((seq_len, HEAD_DIM), jnp.float32)
+        for start in range(0, seq_len, tile):
+            spot = pl.ds(start, tile)
+            grad = attn_grad[spot, head * HEAD_DIM : (head + 1) * HEAD_DIM]
+            prob = probs[head, spot, :]
+            prob_grad = dot(grad, value, 1, 1)
+            inner = jnp.sum(prob * prob_grad, axis=-1, keepdims=True)
+            score_grad = (prob * (prob_grad - inner) * score_scale).astype(jnp.bfloat16)
+            qkv_grad[spot, base : base + HEAD_DIM] = dot(score_grad, key, 1, 0).astype(jnp.bfloat16)
+            key_grad = key_grad + dot(score_grad, query[start : start + tile], 0, 0)
+            value_grad = value_grad + dot(prob.astype(jnp.bfloat16), grad, 0, 0)
+        qkv_grad[:, base + HEAD_DIM : base + 2 * HEAD_DIM] = key_grad.astype(jnp.bfloat16)
+        qkv_grad[:, base + 2 * HEAD_DIM : base + 3 * HEAD_DIM] = value_grad.astype(jnp.bfloat16)
+        if done < outer - 1:
+            ring_step(done, 0, out_set)
+            done += 1
+    make_all(1, in_chunk, in_set)
+    for step in range(done, outer):
+        ring_step(step, 0, out_set)
     for step in range(outer):
-        block = lax.rem(outer_here - step - 1 + outer, outer) * 2
-        for which, (partial, own, pair, _, _, _) in enumerate(arrays):
-            for index in range(pieces):
-                copy = remote(
-                    rows_of(partial, (block + 1 - pair_here) * pieces + index, piece),
-                    pair.at[step, pl.ds(index * piece, piece)],
-                    p_send.at[step, which, index], p_recv.at[step, which, index], partner,
-                )
-                copy.start()
-                pair_copies[step, which, index] = copy
-            load = pltpu.make_async_copy(
-                rows_of(partial, block + pair_here, rows), own.at[step], own_sem.at[step, which]
-            )
-            load.start()
-            loads[step, which] = load
-    for step in range(outer):
-        for which, (_, own, pair, ring, sent, total) in enumerate(arrays):
-            loads[step, which].wait()
-            for index in range(pieces):
-                spot = pl.ds(index * piece, piece)
-                pair_copies[step, which, index].wait_recv()
-                value = own[step, spot, :].astype(jnp.float32) + pair[step, spot, :].astype(jnp.float32)
-                if step > 0:
-                    ring_copies[step - 1, which, index].wait_recv()
-                    value = value + ring[step - 1, spot, :].astype(jnp.float32)
-                if step == outer - 1:
-                    total[spot, :] = value
-                    continue
-                sent[step, spot, :] = value.astype(jnp.bfloat16)
-                copy = remote(
-                    sent.at[step, spot], ring.at[step, spot],
-                    r_send.at[step, which, index], r_recv.at[step, which, index], onward,
-                )
-                copy.start()
-                ring_copies[step, which, index] = copy
+        ring_step(step, 1, in_set)
     for copy in pair_copies.values():
         copy.wait_send()
     for copy in ring_copies.values():
         copy.wait_send()
 
 
-def scatter_all(dp_size, in_partial, out_partial):
-    rows = in_partial.shape[0] // dp_size
-    in_cols, out_cols = in_partial.shape[1], out_partial.shape[1]
+def back_all(dp_size, loss_scale, score_scale, target, attn_rows, out_all, mixed, projected, probs):
+    width, out_cols = out_all.shape
+    rows = width // dp_size
+    in_cols = projected.shape[1]
+    seq_len = target.shape[0]
     low = jnp.bfloat16
     outer = dp_size // 2
+    both = (in_cols, out_cols)
     return pl.pallas_call(
-        functools.partial(scatter_kernel, dp_size),
+        functools.partial(back_kernel, dp_size, loss_scale, score_scale),
         out_shape=(
             jax.ShapeDtypeStruct((rows, in_cols), jnp.float32),
             jax.ShapeDtypeStruct((rows, out_cols), jnp.float32),
         ),
-        in_specs=[HBM, HBM],
+        in_specs=[VMEM] * 6,
         out_specs=(VMEM, VMEM),
-        scratch_shapes=[pltpu.VMEM((outer, rows, cols), low) for _ in range(4) for cols in (in_cols, out_cols)]
-        + [pltpu.SemaphoreType.DMA((outer, 2, 4)) for _ in range(4)]
-        + [pltpu.SemaphoreType.DMA((outer, 2))],
+        scratch_shapes=[pltpu.VMEM((width, cols), jnp.float32) for cols in both]
+        + [pltpu.VMEM((width, cols), low) for cols in both]
+        + [pltpu.VMEM((outer, rows, cols), low) for _ in range(3) for cols in both]
+        + [pltpu.VMEM((seq_len, out_cols), low), pltpu.VMEM((seq_len, in_cols), low)]
+        + [pltpu.SemaphoreType.DMA((outer, 2, 4)) for _ in range(4)],
         compiler_params=pltpu.CompilerParams(
-            collective_id=2, has_side_effects=True, vmem_limit_bytes=32 * 2**20
+            collective_id=2, has_side_effects=True, vmem_limit_bytes=60 * 2**20
         ),
-    )(in_partial, out_partial)
+    )(target, attn_rows, out_all, mixed, projected, probs)
 
 
 def local(dp_size, clean_latents, noise_latents, step_index, labels, class_shift, w_qkv, w_out_t):
@@ -476,15 +545,10 @@
         preferred_element_type=jnp.float32,
     ).astype(jnp.bfloat16)
     target = gather_target(clean, noise, aux, partial)
-    target_wide = target.astype(jnp.float32)
-    spread = jnp.sqrt(jnp.sum(target_wide * target_wide) / (seq_len * model_width))
-    scale = -loss_scale / (spread + target_floor)
-    out_partial = (row_contract(target, attn_rows) * scale).astype(jnp.bfloat16)
-    attn_grad = jnp.dot(target, out_all, preferred_element_type=jnp.float32) * scale
-    attn_grad = attn_grad.astype(jnp.bfloat16).reshape(1, seq_len, heads_here, HEAD_DIM)
-    qkv_grad = attend_back(attn_grad, attn_probs, probs_low, projected, score_scale)
-    in_partial = row_contract(mixed_rows, qkv_grad.reshape(seq_len, 3 * head_cols))
-    return scatter_all(dp_size, in_partial.astype(jnp.bfloat16), out_partial)
+    return back_all(
+        dp_size, loss_scale, score_scale, target, attn_rows, out_all, mixed_rows,
+        projected.reshape(seq_len, 3 * head_cols), attn_probs[0],
+    )
 
 
 def solution(mesh):

time: 182 us -> 166 us (0.912)
  matrix products: 37 us -> 16.7 us
  Pallas kernels: 130 us -> 138 us
    dot_general x9 -> x5, matrix products: 26.1 us -> 7.48 us  [low_einsum(): jnp.einsum(form, left_part, right_part, preferred_element_type=jnp.float32)]
    pallas_call x1, Pallas kernels: 49.3 us -> 55.6 us  [back_all(): pl.pallas_call(functools.partial(back_kernel, dp_size, loss_scale, score_...]
    dot_general x3 -> x0, matrix products: 4.33 us -> none  [the longest x2 3.57 us: row_contract(): lax.dot_general(left_part, right_part, (((0,), (0,)), ((), ())), preferre...]
    dot_general x1, matrix products: 1.78 us -> 4.45 us  [local(): jnp.dot(rate_rows, qkv_all, preferred_element_type=jnp.float32)]
    unnamed x22, local copies, waits for them, and re-layouts: 7.42 us -> 5.27 us
where the time goes in v3:
time: 166 us; the launch traced here: 165 us
  Pallas kernels  138 us (83%)
  matrix products  16.7 us (10%)
  local copies, waits for them, and re-layouts  7.38 us (4%)
  between operations  2.31 us (1%)
    pallas_call x1, Pallas kernels, back_all(): pl.pallas_call(functools.partial(back_kernel, dp_size, loss_scale, score_...  55.6 us
    pallas_call x1, Pallas kernels, gather_all(): pl.pallas_call(functools.partial(gather_kernel, dp_size), out_shape=(jax....  53.9 us
    pallas_call x1, Pallas kernels, gather_target(): pl.pallas_call(target_kernel, out_shape=jax.ShapeDtypeStruct((4 * part, w...  28.3 us
    dot_general x5, matrix products, low_einsum(): jnp.einsum(form, left_part, right_part, preferred_element_type=jnp.float32)  7.48 us
    unnamed x22, local copies, waits for them, and re-layouts  5.27 us
    dot_general x1, matrix products, local(): jnp.dot(rate_rows, qkv_all, preferred_element_type=jnp.float32)  4.45 us

profile of v3, /device:TPU:0, one launch (start us, length us, event | category | flops | bytes accessed | tf_op | source)
XLA Modules:
  0.0 165.2 jit_solution(2197259098026020412)
XLA Ops:
  2.1 0.8 dynamic-slice_convert_fusion
  2.9 0.3 cosine_multiply_fusion
  3.2 0.7 concatenate.3.aux
  3.9 53.9 %shard_map.86 = (bf16[512,2048]{1,0:T(8,128)(2,1)}, bf16[512,2048]{1,0:T(8,128)(2,1)}, bf16[2048,768]{1,0:T(8,128)(2,1)}, bf16[2048,256]{1,0:T(8,128)(2,1)}) custom-call(bf16[128,2048]{1,0:T(8,128)(2,1)} %bitcast.78, bf16[128,2048]{1,0:T(8,128)(2,1)} %bitcast.80, f32[8,2048]{1,0:T(8,128)} %concatenate.3.aux, bf16[256,768]{1,0:T(8,128)(2,1)} %w_qkv.1, ...), custom_call_target="tpu_custom_call" | custom-call | tf_op jit(solution)/shard_map/pallas_call | solution.py:191
  57.7 0.0 copy-start.8
  57.8 0.0 copy-start.9
  57.8 4.5 %convolution_convert_fusion.1 = bf16[512,768]{1,0:T(8,128)(2,1)S(1)} fusion(bf16[512,2048]{1,0:T(8,128)(2,1)} %get-tuple-element.8, bf16[2048,768]{1,0:T(8,128)(2,1)} %get-tuple-element.7), kind=kOutput, calls=%fused_computation.8 | convolution fusion | flops 1611005952 | bytes 6029312 | tf_op jit(solution)/shard_map/dot_general | solution.py:537
  62.2 0.0 copy-done.8
  62.2 0.0 copy-done.9
  62.2 1.8 %convolution_convert_fusion.2.projected = bf16[512,768]{1,0:T(8,128)(2,1)S(1)} fusion(bf16[512,2048]{1,0:T(8,128)(2,1)S(1)} %copy-done.8, bf16[2048,768]{1,0:T(8,128)(2,1)S(1)} %copy-done.9), kind=kOutput, calls=%fused_computation.9 | convolution fusion | flops 1611005952 | bytes 6029312 | tf_op jit(solution)/shard_map/dot_general | solution.py:536
  64.1 0.0 copy-start.6
  64.1 0.3 copy.24
  64.4 0.0 copy-start.7
  64.4 0.3 copy.19
  64.6 1.8 %fusion.11 = f32[2,512,512]{2,1,0:T(8,128)} fusion(bf16[1,512,2,3,128]{1,4,3,2,0:T(8,128)(2,1)S(1)} %bitcast.87, bf16[1,512,2,3,128]{1,4,3,2,0:T(8,128)(2,1)S(1)} %bitcast.82), kind=kOutput, calls=%fused_computation.24 | convolution fusion | flops 134217728 | bytes 2621440 | tf_op jit(solution)/shard_map/lqhd,lkhd->lhqk/dot_general | solution.py:28
  66.5 0.0 copy-done.6
  66.5 2.2 %fusion.14 = (f32[2,512]{1,0:T(2,128)S(1)}, f32[2,512,512]{2,1,0:T(8,128)}) fusion(bf16[1,512,2,3,128]{1,4,3,2,0:T(8,128)(2,1)S(1)} %bitcast.83), kind=kOutput, calls=%fused_computation.35 | convolution fusion | flops 135791104 | bytes 2625536 | tf_op jit(solution)/shard_map/sub | solution.py:43
  68.7 0.0 copy-done.7
  68.7 2.9 %multiply_reduce_fusion = (f32[2,512]{1,0:T(2,128)S(1)}, f32[2,512,512]{2,1,0:T(8,128)S(1)}, f32[2,512,512]{2,1,0:T(8,128)S(1)}) fusion(f32[2,512,512]{2,1,0:T(8,128)} %get-tuple-element.13, f32[2,512]{1,0:T(2,128)S(1)} %get-tuple-element.12, f32[2,512,512]{2,1,0:T(8,128)} %fusion.11, bf16[1,512,2,3,128]{1,4,3,2,0:T(8,128)(2,1)S(1)} %bitcast.88, ...), kind=kOutput, calls=%fused_computation.3 | convolution fusion | flops 136838144 | bytes 8921088 | tf_op jit(solution)/shard_map/lqhd,lkhd->lhqk/dot_general | solution.py:28
  71.6 0.7 fusion.5
  72.3 0.5 fusion.15
  72.8 0.1 copy-done.4
  73.0 1.5 fusion.4
  74.5 0.0 copy-start.1
  74.5 0.0 copy-start.2
  74.5 0.8 copy.34.attn_rows
  75.4 0.8 convolution_convert_fusion.partial
  76.2 28.3 %shard_map.87.target = bf16[512,2048]{1,0:T(8,128)(2,1)S(1)} custom-call(bf16[128,2048]{1,0:T(8,128)(2,1)S(1)} %bitcast.79, bf16[128,2048]{1,0:T(8,128)(2,1)S(1)} %bitcast.81, f32[8,2048]{1,0:T(8,128)S(1)} %copy-done.3, bf16[512,2048]{1,0:T(8,128)(2,1)S(1)} %convolution_convert_fusion.partial), custom_call_target="tpu_custom_call" | custom-call | tf_op jit(solution)/shard_map/pallas_call | solution.py:325
  104.5 1.3 copy-done
  105.8 55.6 %shard_map.88 = (f32[256,768]{1,0:T(8,128)}, f32[256,256]{1,0:T(8,128)}) custom-call(bf16[512,2048]{1,0:T(8,128)(2,1)} %copy-done, bf16[512,256]{1,0:T(8,128)(2,1)} %copy.34.attn_rows, bf16[2048,256]{1,0:T(8,128)(2,1)} %get-tuple-element.9.out_all, bf16[512,2048]{1,0:T(8,128)(2,1)} %get-tuple-element.6.mixed, bf16[512,768]{1,0:T(8,128)(2,1)} %copy-done.6, ...), custom_call_target="tpu_custom_call" | custom-call | tf_op jit(solution)/shard_map/pallas_call | solution.py:493
  161.4 2.1 %copy.45 = f32[256,768]{1,0:T(8,128)} copy(f32[256,768]{1,0:T(8,128)} %get-tuple-element.21) | data formatting | bytes 1572864
  163.5 1.7 %copy.46 = f32[256,256]{1,0:T(8,128)} copy(f32[256,256]{1,0:T(8,128)} %get-tuple-element.22) | data formatting | bytes 524288
  (11 shorter events, 0.0 us)
Async XLA Ops:
  57.7 4.5 %copy-start.8 = (bf16[512,2048]{1,0:T(8,128)(2,1)S(1)}, bf16[512,2048]{1,0:T(8,128)(2,1)}, u32[]{:S(2)}) copy-start(bf16[512,2048]{1,0:T(8,128)(2,1)} %get-tuple-element.6.mixed) | copy-start | bytes 6291460
  57.8 4.5 %copy-start.9 = (bf16[2048,768]{1,0:T(8,128)(2,1)S(1)}, bf16[2048,768]{1,0:T(8,128)(2,1)}, u32[]{:S(2)}) copy-start(bf16[2048,768]{1,0:T(8,128)(2,1)} %get-tuple-element.7) | copy-start | bytes 9437188
  64.1 2.4 %copy-start.6 = (bf16[512,768]{1,0:T(8,128)(2,1)}, bf16[512,768]{1,0:T(8,128)(2,1)S(1)}, u32[]{:S(2)}) copy-start(bf16[512,768]{1,0:T(8,128)(2,1)S(1)} %convolution_convert_fusion.2.projected) | copy-start | bytes 2359300
  64.4 4.3 %copy-start.7 = (bf16[512,768]{0,1:T(8,128)(2,1)}, bf16[512,768]{0,1:T(8,128)(2,1)S(1)}, u32[]{:S(2)}) copy-start(bf16[512,768]{0,1:T(8,128)(2,1)S(1)} %copy.24) | copy-start | bytes 2359300
  71.6 1.4 copy-start.4
  73.0 2.4 %copy-start.5 = (bf16[2048,256]{1,0:T(8,128)(2,1)S(1)}, bf16[2048,256]{1,0:T(8,128)(2,1)}, u32[]{:S(2)}) copy-start(bf16[2048,256]{1,0:T(8,128)(2,1)} %get-tuple-element.9.out_all) | copy-start | bytes 3145732
  74.5 1.6 copy-start.1
  74.5 1.6 copy-start.2
  74.5 1.6 copy-start.3
  104.5 1.4 copy-start

commit v4 on v3

--- a/solution.py
+++ b/solution.py
@@ -22,33 +22,6 @@
     frequency = jnp.exp(-math.log(100.0) * feature_ids / model_width)
     phases = step_times[:, None] * frequency[None, :] + feature_ids[None, :]
     return (step_times, 0.5 * jnp.sin(phases), 0.5 * frequency[None, :] * jnp.cos(phases))
-
-
-def low_einsum(form, left_part, right_part):
-    return jnp.einsum(form, left_part, right_part, preferred_element_type=jnp.float32)
-
-
-def attend(projected, projected_rate, score_scale):
-    query_part = projected[:, :, :, 0, :]
-    key_part = projected[:, :, :, 1, :]
-    value_part = projected[:, :, :, 2, :]
-    query_rate = projected_rate[:, :, :, 0, :]
-    key_rate = projected_rate[:, :, :, 1, :]
-    value_rate = projected_rate[:, :, :, 2, :]
-    scores = low_einsum("lqhd,lkhd->lhqk", query_part, key_part) * score_scale
-    score_rate = (
-        low_einsum("lqhd,lkhd->lhqk", query_rate, key_part)
-        + low_einsum("lqhd,lkhd->lhqk", query_part, key_rate)
-    ) * score_scale
-    attn_probs = jax.nn.softmax(scores, axis=-1)
-    probs_low = attn_probs.astype(jnp.bfloat16)
-    prob_rate = attn_probs * (score_rate - jnp.sum(attn_probs * score_rate, axis=-1, keepdims=True))
-    prob_rate_low = prob_rate.astype(jnp.bfloat16)
-    attn_out = low_einsum("lhqk,lkhd->lqhd", probs_low, value_part)
-    attn_rate = low_einsum("lhqk,lkhd->lqhd", prob_rate_low, value_part) + low_einsum(
-        "lhqk,lkhd->lqhd", probs_low, value_rate
-    )
-    return (attn_probs, probs_low, attn_out, attn_rate)
 
 
 MESH = pl.DeviceIdType.MESH
@@ -86,8 +59,15 @@
     return ref.at[pl.ds(pl.multiple_of(index * count, count), count)]
 
 
+def dot(left, right, left_dim, right_dim):
+    return lax.dot_general(
+        left, right, (((left_dim,), (right_dim,)), ((), ())), preferred_element_type=jnp.float32
+    )
+
+
 def gather_kernel(
-    dp_size, clean, noise, aux, w_qkv, w_out, mixed_all, rate_all, qkv_all, out_all,
+    dp_size, score_scale, clean, noise, aux, w_qkv, w_out, mixed_all, rate_all, qkv_all, out_all,
+    projected, probs, attn_rows, blend, mixed_held, rate_held, qkv_held, projected_rate,
     clean_held, noise_held, mixed, rate, w_send, w_recv, p_send, p_recv, t_send, t_recv, own_sem,
 ):
     dp_here, tensor_here, sibling, opposite, diagonal = places()
@@ -107,27 +87,27 @@
     greet([onward, backward, partner, (dp_here, sibling), (dp_here, opposite)])
     pieces = min(2, qkv_rows // 16)
     piece = qkv_rows // pieces
-    ring_copies, pair_copies = {}, []
-
-    def ring_step(step):
+    ring_copies, pair_copies = {}, {}
+
+    def ring_step(step, which):
         block = lax.rem(outer_here - step + outer, outer) * 2 + pair_here
-        for which, (held, full) in enumerate(((w_qkv, qkv_all), (w_out, out_all))):
-            for index in range(pieces):
-                spot = rows_of(full, block * pieces + index, piece)
-                source = held.at[pl.ds(index * piece, piece)] if step == 0 else spot
-                if step > 0:
-                    ring_copies[step - 1, which, index].wait_recv()
-                if step < outer - 1:
-                    copy = remote(
-                        source, spot, w_send.at[step, which, index], w_recv.at[step, which, index], onward
-                    )
-                    copy.start()
-                    ring_copies[step, which, index] = copy
-                copy = remote(source, spot, p_send.at[step, which, index], p_recv.at[step, which, index], partner)
+        held, full = ((w_qkv, qkv_all), (w_out, out_all))[which]
+        for index in range(pieces):
+            spot = rows_of(full, block * pieces + index, piece)
+            source = held.at[pl.ds(index * piece, piece)] if step == 0 else spot
+            if step > 0:
+                ring_copies[step - 1, which, index].wait_recv()
+            if step < outer - 1:
+                copy = remote(
+                    source, spot, w_send.at[step, which, index], w_recv.at[step, which, index], onward
+                )
                 copy.start()
-                pair_copies.append(copy)
-
-    ring_step(0)
+                ring_copies[step, which, index] = copy
+            copy = remote(source, spot, p_send.at[step, which, index], p_recv.at[step, which, index], partner)
+            copy.start()
+            pair_copies[step, which, index] = copy
+
+    ring_step(0, 0)
     local_copies = [
         pltpu.make_async_copy(w_qkv, rows_of(qkv_all, dp_here, qkv_rows), own_sem.at[0]),
         pltpu.make_async_copy(w_out, rows_of(out_all, dp_here, qkv_rows), own_sem.at[1]),
@@ -169,36 +149,100 @@
         forwards.append(forward)
     for step in range(max(outer - 1, 2)):
         if step + 1 < outer:
-            ring_step(step + 1)
+            ring_step(step + 1, 0)
         if step < 2:
             sends[step][0].wait_recv()
             forwards[step].start()
+    ring_step(0, 1)
+    for copy in local_copies:
+        copy.wait()
+    loads = []
+    for which, (full, held) in enumerate(((mixed_all, mixed_held), (rate_all, rate_held))):
+        sends[which][1].wait_recv()
+        forwards[which].wait_recv()
+        load = pltpu.make_async_copy(full, held, own_sem.at[6 + which])
+        load.start()
+        loads.append(load)
+    for (_, which, _), copy in pair_copies.items():
+        if which == 0:
+            copy.wait_recv()
+    load = pltpu.make_async_copy(qkv_all, qkv_held, own_sem.at[8])
+    load.start()
+    loads.append(load)
+    for load in loads:
+        load.wait()
+    seq_len = mixed_held.shape[0]
+    tile = min(256, seq_len)
+    for step, (held, result) in enumerate(((mixed_held, projected), (rate_held, projected_rate))):
+        for start in range(0, seq_len, tile):
+            spot = pl.ds(start, tile)
+            result[spot, :] = dot(held[spot, :], qkv_held[...], 1, 0).astype(jnp.bfloat16)
+        if step + 1 < outer:
+            ring_step(step + 1, 1)
+    cos_part, sin_part = aux[3:4, :HEAD_DIM], aux[4:5, :HEAD_DIM]
+    done = 3
+    for head in range(probs.shape[0]):
+        base = head * 3 * HEAD_DIM
+        columns = [slice(base + part * HEAD_DIM, base + (part + 1) * HEAD_DIM) for part in range(3)]
+        key, key_rate = projected[:, columns[1]], projected_rate[:, columns[1]]
+        value, value_rate = projected[:, columns[2]], projected_rate[:, columns[2]]
+        here = slice(head * HEAD_DIM, (head + 1) * HEAD_DIM)
+        for start in range(0, seq_len, tile):
+            spot = pl.ds(start, tile)
+            query, query_rate = projected[spot, columns[0]], projected_rate[spot, columns[0]]
+            scores = dot(query, key, 1, 1) * score_scale
+            score_rate = (dot(query_rate, key, 1, 1) + dot(query, key_rate, 1, 1)) * score_scale
+            prob = jnp.exp(scores - jnp.max(scores, axis=-1, keepdims=True))
+            prob = prob * (1.0 / jnp.sum(prob, axis=-1, keepdims=True))
+            inner = jnp.sum(prob * score_rate, axis=-1, keepdims=True)
+            prob_rate = (prob * (score_rate - inner)).astype(jnp.bfloat16)
+            probs[head, spot, :] = prob
+            prob_low = prob.astype(jnp.bfloat16)
+            attn = dot(prob_low, value, 1, 0)
+            attn_rate = dot(prob_rate, value, 1, 0) + dot(prob_low, value_rate, 1, 0)
+            attn_rows[spot, here] = attn.astype(jnp.bfloat16)
+            mix = cos_part * cos_part * attn + cos_part * sin_part * attn_rate
+            blend[spot, here] = mix.astype(jnp.bfloat16)
+        if done < outer:
+            ring_step(done, 1)
+            done += 1
+    for step in range(done, outer):
+        ring_step(step, 1)
     for (to_opposite, to_sibling), forward in zip(sends, forwards):
         to_opposite.wait_send()
-        to_sibling.wait()
-        forward.wait()
+        to_sibling.wait_send()
+        forward.wait_send()
     for copy in ring_copies.values():
         copy.wait_send()
-    for copy in pair_copies:
-        copy.wait()
-    for copy in local_copies:
-        copy.wait()
-
-
-def gather_all(dp_size, clean, noise, aux, w_qkv, w_out):
+    for (_, which, _), copy in pair_copies.items():
+        copy.wait_send()
+        if which == 1:
+            copy.wait_recv()
+
+
+def gather_all(dp_size, score_scale, clean, noise, aux, w_qkv, w_out):
     part, width = clean.shape
     low = jnp.bfloat16
+    seq_len, cols, head_cols = 4 * part, w_qkv.shape[1], w_out.shape[1]
     return pl.pallas_call(
-        functools.partial(gather_kernel, dp_size),
+        functools.partial(gather_kernel, dp_size, score_scale),
         out_shape=(
             jax.ShapeDtypeStruct((4 * part, width), low),
             jax.ShapeDtypeStruct((4 * part, width), low),
             jax.ShapeDtypeStruct((dp_size * w_qkv.shape[0], w_qkv.shape[1]), low),
             jax.ShapeDtypeStruct((dp_size * w_out.shape[0], w_out.shape[1]), low),
+            jax.ShapeDtypeStruct((seq_len, cols), low),
+            jax.ShapeDtypeStruct((head_cols // HEAD_DIM, seq_len, seq_len), jnp.float32),
+            jax.ShapeDtypeStruct((seq_len, head_cols), low),
+            jax.ShapeDtypeStruct((seq_len, head_cols), low),
         ),
         in_specs=[HBM, HBM, VMEM, HBM, HBM],
-        out_specs=(HBM,) * 4,
+        out_specs=(HBM,) * 4 + (VMEM,) * 4,
         scratch_shapes=[
+            pltpu.VMEM((seq_len, width), low),
+            pltpu.VMEM((seq_len, width), low),
+            pltpu.VMEM((dp_size * w_qkv.shape[0], cols), low),
+            pltpu.VMEM((seq_len, cols), low),
             pltpu.VMEM((part, width), low),
             pltpu.VMEM((part, width), low),
             pltpu.VMEM((part, width), low),
@@ -209,7 +253,7 @@
             pltpu.SemaphoreType.DMA((dp_size // 2, 2, 2)),
             pltpu.SemaphoreType.DMA((2, 3)),
             pltpu.SemaphoreType.DMA((2, 3)),
-            pltpu.SemaphoreType.DMA((6,)),
+            pltpu.SemaphoreType.DMA((9,)),
         ],
         compiler_params=pltpu.CompilerParams(
             collective_id=0, has_side_effects=True, vmem_limit_bytes=60 * 2**20
@@ -343,12 +387,6 @@
             collective_id=1, has_side_effects=True, vmem_limit_bytes=32 * 2**20
         ),
     )(clean, noise, aux, partial)
-
-
-def dot(left, right, left_dim, right_dim):
-    return lax.dot_general(
-        left, right, (((left_dim,), (right_dim,)), ((), ())), preferred_element_type=jnp.float32
-    )
 
 
 def back_kernel(
@@ -511,8 +549,6 @@
 
 def local(dp_size, clean_latents, noise_latents, step_index, labels, class_shift, w_qkv, w_out_t):
     latent_count, part_len, model_width = clean_latents.shape
-    head_cols = w_out_t.shape[1]
-    heads_here = head_cols // HEAD_DIM
     score_scale = 1.0 / math.sqrt(HEAD_DIM)
     seq_len = part_len * 4
     loss_scale = 1.0 / math.sqrt(dp_size * latent_count * seq_len)
@@ -531,23 +567,15 @@
         ]
     )
     clean, noise = clean_latents[0], noise_latents[0]
-    mixed_rows, rate_rows, qkv_all, out_all = gather_all(dp_size, clean, noise, aux, w_qkv, w_out_t)
-    heads_shape = (1, seq_len, heads_here, 3, HEAD_DIM)
-    projected = jnp.dot(mixed_rows, qkv_all, preferred_element_type=jnp.float32)
-    projected_rate = jnp.dot(rate_rows, qkv_all, preferred_element_type=jnp.float32)
-    projected = projected.astype(jnp.bfloat16).reshape(heads_shape)
-    projected_rate = projected_rate.astype(jnp.bfloat16).reshape(heads_shape)
-    attn_probs, probs_low, attn_out, attn_rate = attend(projected, projected_rate, score_scale)
-    attn_rows = attn_out.astype(jnp.bfloat16).reshape(seq_len, head_cols)
-    blend = (cos_t * cos_t * attn_out + cos_t * sin_t * attn_rate).astype(jnp.bfloat16)
+    mixed_rows, _, _, out_all, projected, probs, attn_rows, blend = gather_all(
+        dp_size, score_scale, clean, noise, aux, w_qkv, w_out_t
+    )
     partial = lax.dot_general(
-        blend.reshape(seq_len, head_cols), out_all, (((1,), (1,)), ((), ())),
-        preferred_element_type=jnp.float32,
+        blend, out_all, (((1,), (1,)), ((), ())), preferred_element_type=jnp.float32
     ).astype(jnp.bfloat16)
     target = gather_target(clean, noise, aux, partial)
     return back_all(
-        dp_size, loss_scale, score_scale, target, attn_rows, out_all, mixed_rows,
-        projected.reshape(seq_len, 3 * head_cols), attn_probs[0],
+        dp_size, loss_scale, score_scale, target, attn_rows, out_all, mixed_rows, projected, probs
     )
 
 

time: 166 us -> 157 us (0.946)
  matrix products: 16.7 us -> 2.13 us
  Pallas kernels: 138 us -> 145 us
    dot_general x8 -> x1, matrix products: 14.5 us -> 2.13 us  [local(): lax.dot_general(blend, out_all, (((1,), (1,)), ((), ())), preferred_eleme...]
    pallas_call x1, Pallas kernels: 53.9 us -> 60.4 us  [gather_all(): pl.pallas_call(functools.partial(gather_kernel, dp_size, score_scale), ou...]
    sub x1 -> x0, matrix products: 2.18 us -> none  [attend(): attn_probs = jax.nn.softmax(scores, axis=-1)]
    unnamed x22 -> x10, local copies, waits for them, and re-layouts: 5.27 us -> 5.1 us
where the time goes in v4:
time: 157 us; the launch traced here: 156 us
  Pallas kernels  145 us (92%)
  local copies, waits for them, and re-layouts  5.82 us (4%)
  between operations  2.2 us (1%)
  matrix products  2.13 us (1%)
    pallas_call x1, Pallas kernels, gather_all(): pl.pallas_call(functools.partial(gather_kernel, dp_size, score_scale), ou...  60.4 us
    pallas_call x1, Pallas kernels, back_all(): pl.pallas_call(functools.partial(back_kernel, dp_size, loss_scale, score_...  56.2 us
    pallas_call x1, Pallas kernels, gather_target(): pl.pallas_call(target_kernel, out_shape=jax.ShapeDtypeStruct((4 * part, w...  28.6 us
    unnamed x10, local copies, waits for them, and re-layouts  5.1 us

profile of v4, /device:TPU:0, one launch (start us, length us, event | category | flops | bytes accessed | tf_op | source)
XLA Modules:
  0.0 156.4 jit_solution(13562220391108300807)
XLA Ops:
  2.1 0.8 dynamic-slice_convert_fusion
  2.9 0.3 cosine_multiply_fusion
  3.2 0.7 concatenate.3.aux
  3.9 60.4 %shard_map.86 = (bf16[512,2048]{1,0:T(8,128)(2,1)}, bf16[512,2048]{1,0:T(8,128)(2,1)}, bf16[2048,768]{1,0:T(8,128)(2,1)}, bf16[2048,256]{1,0:T(8,128)(2,1)}, bf1...) custom-call(bf16[128,2048]{1,0:T(8,128)(2,1)} %bitcast.9, ...), custom_call_target="tpu_custom_call" | custom-call | tf_op jit(solution)/shard_map/pallas_call | solution.py:227
  64.3 0.0 copy-start.1
  64.3 0.0 copy-start.2
  64.3 0.0 copy-start.3
  64.4 2.1 %convolution_convert_fusion.partial = bf16[512,2048]{1,0:T(8,128)(2,1)S(1)} fusion(bf16[512,256]{1,0:T(8,128)(2,1)} %get-tuple-element.8, bf16[2048,256]{1,0:T(8,128)(2,1)} %get-tuple-element.9.out_all), kind=kOutput, calls=%fused_computation | convolution fusion | flops 537919488 | bytes 3407872 | tf_op jit(solution)/shard_map/dot_general | solution.py:573
  66.5 0.0 copy-done.1
  66.5 0.0 copy-done.2
  66.5 0.0 copy-done.3
  66.5 28.6 %shard_map.87.target = bf16[512,2048]{1,0:T(8,128)(2,1)S(1)} custom-call(bf16[128,2048]{1,0:T(8,128)(2,1)S(1)} %bitcast.10, bf16[128,2048]{1,0:T(8,128)(2,1)S(1)} %bitcast.12, f32[8,2048]{1,0:T(8,128)S(1)} %copy-done.3, bf16[512,2048]{1,0:T(8,128)(2,1)S(1)} %convolution_convert_fusion.partial), custom_call_target="tpu_custom_call" | custom-call | tf_op jit(solution)/shard_map/pallas_call | solution.py:369
  95.1 0.0 copy-start
  95.1 1.3 copy-done
  96.5 56.2 %shard_map.88 = (f32[256,768]{1,0:T(8,128)}, f32[256,256]{1,0:T(8,128)}) custom-call(bf16[512,2048]{1,0:T(8,128)(2,1)} %copy-done, bf16[512,256]{1,0:T(8,128)(2,1)} %get-tuple-element.10.attn_rows, bf16[2048,256]{1,0:T(8,128)(2,1)} %get-tuple-element.9.out_all, bf16[512,2048]{1,0:T(8,128)(2,1)} %get-tuple-element.11.mixed, ...), custom_call_target="tpu_custom_call" | custom-call | tf_op jit(solution)/shard_map/pallas_call | solution.py:531
  152.7 2.1 %copy.13 = f32[256,768]{1,0:T(8,128)} copy(f32[256,768]{1,0:T(8,128)} %get-tuple-element.18) | data formatting | bytes 1572864
  154.7 1.7 %copy.14 = f32[256,256]{1,0:T(8,128)} copy(f32[256,256]{1,0:T(8,128)} %get-tuple-element.19) | data formatting | bytes 524288
  (3 shorter events, 0.0 us)
Async XLA Ops:
  64.3 2.2 %copy-start.1 = (bf16[1,128,2048]{2,1,0:T(8,128)(2,1)S(1)}, bf16[1,128,2048]{2,1,0:T(8,128)(2,1)}, u32[]{:S(2)}) copy-start(bf16[1,128,2048]{2,1,0:T(8,128)(2,1)} %param.7) | copy-start | bytes 1572868
  64.3 2.2 %copy-start.2 = (bf16[1,128,2048]{2,1,0:T(8,128)(2,1)S(1)}, bf16[1,128,2048]{2,1,0:T(8,128)(2,1)}, u32[]{:S(2)}) copy-start(bf16[1,128,2048]{2,1,0:T(8,128)(2,1)} %param.8) | copy-start | bytes 1572868
  64.3 2.2 %copy-start.3 = (f32[8,2048]{1,0:T(8,128)S(1)}, f32[8,2048]{1,0:T(8,128)}, u32[]{:S(2)}) copy-start(f32[8,2048]{1,0:T(8,128)} %concatenate.3.aux) | copy-start | bytes 196612
  95.1 1.4 copy-start

commit v5 on v4

--- a/solution.py
+++ b/solution.py
@@ -261,7 +261,7 @@
     )(clean, noise, aux, w_qkv, w_out)
 
 
-PIECES = 4
+PIECES = 8
 
 
 def target_kernel(
@@ -542,7 +542,7 @@
         + [pltpu.VMEM((seq_len, out_cols), low), pltpu.VMEM((seq_len, in_cols), low)]
         + [pltpu.SemaphoreType.DMA((outer, 2, 4)) for _ in range(4)],
         compiler_params=pltpu.CompilerParams(
-            collective_id=2, has_side_effects=True, vmem_limit_bytes=60 * 2**20
+            collective_id=2, has_side_effects=True, vmem_limit_bytes=36 * 2**20
         ),
     )(target, attn_rows, out_all, mixed, projected, probs)
 

time: 157 us -> 149 us (0.949)
  Pallas kernels: 145 us -> 141 us
  local copies, waits for them, and re-layouts: 5.82 us -> 2.35 us
    pallas_call x1, Pallas kernels: 56.2 us -> 51.7 us  [back_all(): pl.pallas_call(functools.partial(back_kernel, dp_size, loss_scale, score_...]
    unnamed x10 -> x18, local copies, waits for them, and re-layouts: 5.1 us -> 1.62 us
where the time goes in v5:
time: 149 us
  Pallas kernels  141 us (95%)
  local copies, waits for them, and re-layouts  2.35 us (2%)
  between operations  2.27 us (2%)
  matrix products  2.19 us (1%)
    pallas_call x1, Pallas kernels, gather_all(): pl.pallas_call(functools.partial(gather_kernel, dp_size, score_scale), ou...  60.4 us
    pallas_call x1, Pallas kernels, back_all(): pl.pallas_call(functools.partial(back_kernel, dp_size, loss_scale, score_...  51.7 us
    pallas_call x1, Pallas kernels, gather_target(): pl.pallas_call(target_kernel, out_shape=jax.ShapeDtypeStruct((4 * part, w...  29.1 us

profile of v5, /device:TPU:0, one launch (start us, length us, event | category | flops | bytes accessed | tf_op | source)
XLA Modules:
  0.0 149.1 jit_solution(16825253704498548932)
XLA Ops:
  2.1 0.8 dynamic-slice_convert_fusion
  2.9 0.3 cosine_multiply_fusion
  3.2 0.7 concatenate.3.aux
  3.9 60.4 %shard_map.86 = (bf16[512,2048]{1,0:T(8,128)(2,1)}, bf16[512,2048]{1,0:T(8,128)(2,1)}, bf16[2048,768]{1,0:T(8,128)(2,1)}, bf16[2048,256]{1,0:T(8,128)(2,1)}, bf1...) custom-call(bf16[128,2048]{1,0:T(8,128)(2,1)} %bitcast.9, ...), custom_call_target="tpu_custom_call" | custom-call | tf_op jit(solution)/shard_map/pallas_call | solution.py:227
  64.3 0.0 copy-start.3
  64.3 0.0 copy-start.4
  64.3 0.0 copy-start.6
  64.3 0.0 copy-start.5
  64.4 0.0 copy-start.7
  64.4 2.2 %convolution_convert_fusion.partial = bf16[512,2048]{1,0:T(8,128)(2,1)S(1)} fusion(bf16[512,256]{1,0:T(8,128)(2,1)} %get-tuple-element.8, bf16[2048,256]{1,0:T(8,128)(2,1)} %get-tuple-element.9.out_all), kind=kOutput, calls=%fused_computation | convolution fusion | flops 537919488 | bytes 3407872 | tf_op jit(solution)/shard_map/dot_general | solution.py:573
  66.6 0.0 copy-done.3
  66.6 0.0 copy-done.4
  66.6 0.0 copy-done.6
  66.6 0.0 copy-start
  66.6 0.0 copy-start.1
  66.6 0.0 copy-start.2
  66.6 29.1 %shard_map.87.target = bf16[512,2048]{1,0:T(8,128)(2,1)S(1)} custom-call(bf16[128,2048]{1,0:T(8,128)(2,1)S(1)} %bitcast.10, bf16[128,2048]{1,0:T(8,128)(2,1)S(1)} %bitcast.12, f32[8,2048]{1,0:T(8,128)S(1)} %copy-done.6, bf16[512,2048]{1,0:T(8,128)(2,1)S(1)} %convolution_convert_fusion.partial), custom_call_target="tpu_custom_call" | custom-call | tf_op jit(solution)/shard_map/pallas_call | solution.py:369
  95.7 0.0 copy-done.5
  95.7 0.0 copy-done.7
  95.7 0.0 copy-done
  95.7 0.0 copy-done.1
  95.7 0.0 copy-done.2
  95.7 51.7 %shard_map.88 = (f32[256,768]{1,0:T(8,128)S(1)}, f32[256,256]{1,0:T(8,128)S(1)}) custom-call(bf16[512,2048]{1,0:T(8,128)(2,1)S(1)} %shard_map.87.target, bf16[512,256]{1,0:T(8,128)(2,1)S(1)} %copy-done.7, bf16[2048,256]{1,0:T(8,128)(2,1)S(1)} %copy-done, bf16[512,2048]{1,0:T(8,128)(2,1)S(1)} %copy-done.1, bf16[512,768]{1,0:T(8,128)(2,1)S(1)} %copy-done.5, ...), custom_call_target="tpu_custom_call" | custom-call | tf_op jit(solution)/shard_map/pallas_call | solution.py:531
  147.5 0.9 copy.13
  148.4 0.7 copy.14
  (3 shorter events, 0.0 us)
Async XLA Ops:
  64.3 2.3 %copy-start.3 = (bf16[1,128,2048]{2,1,0:T(8,128)(2,1)S(1)}, bf16[1,128,2048]{2,1,0:T(8,128)(2,1)}, u32[]{:S(2)}) copy-start(bf16[1,128,2048]{2,1,0:T(8,128)(2,1)} %param.7) | copy-start | bytes 1572868
  64.3 2.3 %copy-start.4 = (bf16[1,128,2048]{2,1,0:T(8,128)(2,1)S(1)}, bf16[1,128,2048]{2,1,0:T(8,128)(2,1)}, u32[]{:S(2)}) copy-start(bf16[1,128,2048]{2,1,0:T(8,128)(2,1)} %param.8) | copy-start | bytes 1572868
  64.3 2.3 %copy-start.6 = (f32[8,2048]{1,0:T(8,128)S(1)}, f32[8,2048]{1,0:T(8,128)}, u32[]{:S(2)}) copy-start(f32[8,2048]{1,0:T(8,128)} %concatenate.3.aux) | copy-start | bytes 196612
  64.3 31.3 %copy-start.5 = (bf16[512,768]{1,0:T(8,128)(2,1)S(1)}, bf16[512,768]{1,0:T(8,128)(2,1)}, u32[]{:S(2)}) copy-start(bf16[512,768]{1,0:T(8,128)(2,1)} %get-tuple-element.12.projected) | copy-start | bytes 2359300
  64.4 31.3 %copy-start.7 = (bf16[512,256]{1,0:T(8,128)(2,1)S(1)}, bf16[512,256]{1,0:T(8,128)(2,1)}, u32[]{:S(2)}) copy-start(bf16[512,256]{1,0:T(8,128)(2,1)} %get-tuple-element.10.attn_rows) | copy-start | bytes 786436
  66.6 29.1 %copy-start = (bf16[2048,256]{1,0:T(8,128)(2,1)S(1)}, bf16[2048,256]{1,0:T(8,128)(2,1)}, u32[]{:S(2)}) copy-start(bf16[2048,256]{1,0:T(8,128)(2,1)} %get-tuple-element.9.out_all) | copy-start | bytes 3145732
  66.6 29.1 %copy-start.1 = (bf16[512,2048]{1,0:T(8,128)(2,1)S(1)}, bf16[512,2048]{1,0:T(8,128)(2,1)}, u32[]{:S(2)}) copy-start(bf16[512,2048]{1,0:T(8,128)(2,1)} %get-tuple-element.11.mixed) | copy-start | bytes 6291460
  66.6 29.1 %copy-start.2 = (f32[2,512,512]{2,1,0:T(8,128)S(1)}, f32[2,512,512]{2,1,0:T(8,128)}, u32[]{:S(2)}) copy-start(f32[2,512,512]{2,1,0:T(8,128)} %get-tuple-element.13.probs) | copy-start | bytes 6291460

commit v6 on v5

--- a/solution.py
+++ b/solution.py
@@ -85,7 +85,7 @@
     backward = (lax.rem(outer_here + outer - 1, outer) * 2 + pair_here, tensor_here)
     partner = (outer_here * 2 + 1 - pair_here, tensor_here)
     greet([onward, backward, partner, (dp_here, sibling), (dp_here, opposite)])
-    pieces = min(2, qkv_rows // 16)
+    pieces = min(4, qkv_rows // 16)
     piece = qkv_rows // pieces
     ring_copies, pair_copies = {}, {}
 
@@ -247,10 +247,10 @@
             pltpu.VMEM((part, width), low),
             pltpu.VMEM((part, width), low),
             pltpu.VMEM((part, width), low),
-            pltpu.SemaphoreType.DMA((dp_size // 2, 2, 2)),
-            pltpu.SemaphoreType.DMA((dp_size // 2, 2, 2)),
-            pltpu.SemaphoreType.DMA((dp_size // 2, 2, 2)),
-            pltpu.SemaphoreType.DMA((dp_size // 2, 2, 2)),
+            pltpu.SemaphoreType.DMA((dp_size // 2, 2, 4)),
+            pltpu.SemaphoreType.DMA((dp_size // 2, 2, 4)),
+            pltpu.SemaphoreType.DMA((dp_size // 2, 2, 4)),
+            pltpu.SemaphoreType.DMA((dp_size // 2, 2, 4)),
             pltpu.SemaphoreType.DMA((2, 3)),
             pltpu.SemaphoreType.DMA((2, 3)),
             pltpu.SemaphoreType.DMA((9,)),
@@ -261,7 +261,7 @@
     )(clean, noise, aux, w_qkv, w_out)
 
 
-PIECES = 8
+PIECES = 4
 
 
 def target_kernel(

time: 149 us -> 148 us (level)
  no operation moved by 1% of the time
where the time goes in v6:
time: 148 us
  Pallas kernels  140 us (95%)
  local copies, waits for them, and re-layouts  2.35 us (2%)
  between operations  2.27 us (2%)
  matrix products  2.19 us (1%)
    pallas_call x1, Pallas kernels, gather_all(): pl.pallas_call(functools.partial(gather_kernel, dp_size, score_scale), ou...  60.3 us
    pallas_call x1, Pallas kernels, back_all(): pl.pallas_call(functools.partial(back_kernel, dp_size, loss_scale, score_...  51.5 us
    pallas_call x1, Pallas kernels, gather_target(): pl.pallas_call(target_kernel, out_shape=jax.ShapeDtypeStruct((4 * part, w...  28.5 us

profile of v6, /device:TPU:0, one launch (start us, length us, event | category | flops | bytes accessed | tf_op | source)
XLA Modules:
  0.0 148.1 jit_solution(133490997718434804)
XLA Ops:
  2.1 0.8 dynamic-slice_convert_fusion
  2.9 0.3 cosine_multiply_fusion
  3.2 0.7 concatenate.3.aux
  3.9 60.3 %shard_map.86 = (bf16[512,2048]{1,0:T(8,128)(2,1)}, bf16[512,2048]{1,0:T(8,128)(2,1)}, bf16[2048,768]{1,0:T(8,128)(2,1)}, bf16[2048,256]{1,0:T(8,128)(2,1)}, bf1...) custom-call(bf16[128,2048]{1,0:T(8,128)(2,1)} %bitcast.9, ...), custom_call_target="tpu_custom_call" | custom-call | tf_op jit(solution)/shard_map/pallas_call | solution.py:227
  64.2 0.0 copy-start.3
  64.2 0.0 copy-start.4
  64.2 0.0 copy-start.6
  64.2 0.0 copy-start.5
  64.2 0.0 copy-start.7
  64.2 2.2 %convolution_convert_fusion.partial = bf16[512,2048]{1,0:T(8,128)(2,1)S(1)} fusion(bf16[512,256]{1,0:T(8,128)(2,1)} %get-tuple-element.8, bf16[2048,256]{1,0:T(8,128)(2,1)} %get-tuple-element.9.out_all), kind=kOutput, calls=%fused_computation | convolution fusion | flops 537919488 | bytes 3407872 | tf_op jit(solution)/shard_map/dot_general | solution.py:573
  66.4 0.0 copy-done.3
  66.4 0.0 copy-done.4
  66.5 0.0 copy-done.6
  66.5 0.0 copy-start
  66.5 0.0 copy-start.1
  66.5 0.0 copy-start.2
  66.5 28.5 %shard_map.87.target = bf16[512,2048]{1,0:T(8,128)(2,1)S(1)} custom-call(bf16[128,2048]{1,0:T(8,128)(2,1)S(1)} %bitcast.10, bf16[128,2048]{1,0:T(8,128)(2,1)S(1)} %bitcast.12, f32[8,2048]{1,0:T(8,128)S(1)} %copy-done.6, bf16[512,2048]{1,0:T(8,128)(2,1)S(1)} %convolution_convert_fusion.partial), custom_call_target="tpu_custom_call" | custom-call | tf_op jit(solution)/shard_map/pallas_call | solution.py:369
  95.0 0.0 copy-done.5
  95.0 0.0 copy-done.7
  95.0 0.0 copy-done
  95.0 0.0 copy-done.1
  95.1 0.0 copy-done.2
  95.1 51.5 %shard_map.88 = (f32[256,768]{1,0:T(8,128)S(1)}, f32[256,256]{1,0:T(8,128)S(1)}) custom-call(bf16[512,2048]{1,0:T(8,128)(2,1)S(1)} %shard_map.87.target, bf16[512,256]{1,0:T(8,128)(2,1)S(1)} %copy-done.7, bf16[2048,256]{1,0:T(8,128)(2,1)S(1)} %copy-done, bf16[512,2048]{1,0:T(8,128)(2,1)S(1)} %copy-done.1, bf16[512,768]{1,0:T(8,128)(2,1)S(1)} %copy-done.5, ...), custom_call_target="tpu_custom_call" | custom-call | tf_op jit(solution)/shard_map/pallas_call | solution.py:531
  146.5 0.9 copy.13
  147.4 0.7 copy.14
  (3 shorter events, 0.0 us)
Async XLA Ops:
  64.2 2.3 %copy-start.3 = (bf16[1,128,2048]{2,1,0:T(8,128)(2,1)S(1)}, bf16[1,128,2048]{2,1,0:T(8,128)(2,1)}, u32[]{:S(2)}) copy-start(bf16[1,128,2048]{2,1,0:T(8,128)(2,1)} %param.7) | copy-start | bytes 1572868
  64.2 2.3 %copy-start.4 = (bf16[1,128,2048]{2,1,0:T(8,128)(2,1)S(1)}, bf16[1,128,2048]{2,1,0:T(8,128)(2,1)}, u32[]{:S(2)}) copy-start(bf16[1,128,2048]{2,1,0:T(8,128)(2,1)} %param.8) | copy-start | bytes 1572868
  64.2 2.3 %copy-start.6 = (f32[8,2048]{1,0:T(8,128)S(1)}, f32[8,2048]{1,0:T(8,128)}, u32[]{:S(2)}) copy-start(f32[8,2048]{1,0:T(8,128)} %concatenate.3.aux) | copy-start | bytes 196612
  64.2 30.8 %copy-start.5 = (bf16[512,768]{1,0:T(8,128)(2,1)S(1)}, bf16[512,768]{1,0:T(8,128)(2,1)}, u32[]{:S(2)}) copy-start(bf16[512,768]{1,0:T(8,128)(2,1)} %get-tuple-element.12.projected) | copy-start | bytes 2359300
  64.2 30.8 %copy-start.7 = (bf16[512,256]{1,0:T(8,128)(2,1)S(1)}, bf16[512,256]{1,0:T(8,128)(2,1)}, u32[]{:S(2)}) copy-start(bf16[512,256]{1,0:T(8,128)(2,1)} %get-tuple-element.10.attn_rows) | copy-start | bytes 786436
  66.5 28.6 %copy-start = (bf16[2048,256]{1,0:T(8,128)(2,1)S(1)}, bf16[2048,256]{1,0:T(8,128)(2,1)}, u32[]{:S(2)}) copy-start(bf16[2048,256]{1,0:T(8,128)(2,1)} %get-tuple-element.9.out_all) | copy-start | bytes 3145732
  66.5 28.6 %copy-start.1 = (bf16[512,2048]{1,0:T(8,128)(2,1)S(1)}, bf16[512,2048]{1,0:T(8,128)(2,1)}, u32[]{:S(2)}) copy-start(bf16[512,2048]{1,0:T(8,128)(2,1)} %get-tuple-element.11.mixed) | copy-start | bytes 6291460
  66.5 28.6 %copy-start.2 = (f32[2,512,512]{2,1,0:T(8,128)S(1)}, f32[2,512,512]{2,1,0:T(8,128)}, u32[]{:S(2)}) copy-start(f32[2,512,512]{2,1,0:T(8,128)} %get-tuple-element.13.probs) | copy-start | bytes 6291460
